TPU v7x, 32 devices: a whole 2x2x4 slice. The times are simulated.
32 devices in a mesh: batch: 2 (over x), ctx: 4 (over z), seq: 4 (over y, core).
Axes of the slice: x: 2, y: 2, z: 4, core: 2. Of those that a mesh axis runs over, the one named last changes fastest.
Arguments:
- hidden: bfloat16 [32, 6144], P('batch'), parts along dimension 0
- lengths: int32 [32], P('batch'), parts along dimension 0
- latent_cache: bfloat16 [32, 8192, 512], P('batch', ('ctx', 'seq')), parts along dimension 0
- rope_keys: bfloat16 [32, 8192, 64], P('batch', ('ctx', 'seq')), parts along dimension 0
- w_uq: bfloat16 [6144, 64, 128], P(None, 'seq')
- w_qr: bfloat16 [6144, 64, 64], P(None, 'seq')
- w_uk: bfloat16 [64, 128, 512], P('seq')
- w_uv: bfloat16 [64, 512, 128], P('seq')
- w_out: bfloat16 [64, 128, 6144], P('seq')
Outputs:
- output: bfloat16 [32, 6144], P('batch'), parts along dimension 0
There are 2 independent parts. A program takes and returns all parts, laid end to end along the dimension named above; an argument that names none is the same for every part.
All inputs are finite; a program needn't handle non-finite values.
Results may differ from a plain program's by a relative error of at most 0.00548613.
Values are sent between devices in bfloat16 or wider.
A program may use at most 1 GiB of HBM per device.

v0:
```python
import jax
import jax.numpy as jnp
from jax import lax
from jax.sharding import PartitionSpec as P

NEG_FILL = -1.0e30


def solution(mesh):
    seq_size = mesh.shape['seq']
    row_spec = P('batch', None)
    cache_spec = P('batch', ('ctx', 'seq'), None)
    proj_spec = P(None, 'seq', None)
    head_spec = P('seq', None, None)

    def local_step(hidden, lengths, latent_cache, rope_keys, w_uq, w_qr, w_uk, w_uv, w_out):
        t_local = latent_cache.shape[1]
        score_scale = (w_uq.shape[2] + w_qr.shape[2]) ** -0.5
        q_nope = jnp.einsum('bd,dhk->bhk', hidden, w_uq, preferred_element_type=jnp.float32).astype(jnp.bfloat16)
        q_rope = jnp.einsum('bd,dhr->bhr', hidden, w_qr, preferred_element_type=jnp.float32).astype(jnp.bfloat16)
        q_lat = jnp.einsum('bhk,hkc->bhc', q_nope, w_uk, preferred_element_type=jnp.float32).astype(jnp.bfloat16)
        lat_all = lax.all_gather(q_lat, 'seq', axis=1, tiled=True)
        rope_all = lax.all_gather(q_rope, 'seq', axis=1, tiled=True)
        scores = jnp.einsum('bhc,btc->bht', lat_all, latent_cache, preferred_element_type=jnp.float32)
        scores = (scores + jnp.einsum('bhr,btr->bht', rope_all, rope_keys, preferred_element_type=jnp.float32)) * score_scale
        shard_index = lax.axis_index('ctx') * seq_size + lax.axis_index('seq')
        positions = shard_index * t_local + jnp.arange(t_local)
        valid = positions[None, None, :] < lengths[:, None, None]
        scores = jnp.where(valid, scores, NEG_FILL)
        local_max = jnp.max(scores, axis=2)
        weights = jnp.where(valid, jnp.exp(scores - local_max[:, :, None]), 0.0)
        local_sum = jnp.sum(weights, axis=2)
        local_acc = jnp.einsum('bht,btc->bhc', weights.astype(jnp.bfloat16), latent_cache, preferred_element_type=jnp.float32)
        global_max = lax.pmax(local_max, ('ctx', 'seq'))
        rescale = jnp.exp(local_max - global_max)
        acc_heads = lax.psum_scatter(local_acc * rescale[:, :, None], 'seq', scatter_dimension=1, tiled=True)
        sum_heads = lax.psum_scatter(local_sum * rescale, 'seq', scatter_dimension=1, tiled=True)
        acc_heads = lax.psum(acc_heads, 'ctx')
        sum_heads = lax.psum(sum_heads, 'ctx')
        lat_out = (acc_heads / sum_heads[:, :, None]).astype(jnp.bfloat16)
        head_vals = jnp.einsum('bhc,hcv->bhv', lat_out, w_uv, preferred_element_type=jnp.float32).astype(jnp.bfloat16)
        mixed_part = jnp.einsum('bhv,hvd->bd', head_vals, w_out, preferred_element_type=jnp.float32)
        mixed = lax.psum(mixed_part, 'seq')
        return (hidden.astype(jnp.float32) + mixed).astype(jnp.bfloat16)

    return jax.shard_map(local_step, mesh=mesh,
                         in_specs=(row_spec, P('batch'), cache_spec, cache_spec, proj_spec, proj_spec, head_spec, head_spec, head_spec),
                         out_specs=row_spec, check_vma=False)
```

profile of v0, /device:TPU:0, one launch (start us, length us, event | category | flops | bytes accessed | tf_op | source)
XLA Modules:
  0.0 232.9 jit_solution(9084292732556106787)
XLA Ops:
  6.5 11.7 %fusion = bf16[16,16,128]{2,0,1:T(8,128)(2,1)S(1)} fusion(bf16[6144,16,128]{2,1,0:T(8,128)(2,1)} %param.13, bf16[16,6144]{1,0:T(8,128)(2,1)} %param.9), kind=kOutput, calls=%fused_computation | convolution fusion | flops 402653184 | bytes 25427968 | tf_op jit(solution)/shard_map/bd,dhk->bhk/dot_general | solution.py:19
  18.3 0.4 fusion.15
  18.7 0.9 copy.32
  19.6 0.0 all-gather.2.cloned.1.call-update
  19.6 0.0 reduce-scatter.5.cloned.1.call-start
  19.6 0.0 copy-start.4
  19.7 8.0 %fusion.12 = bf16[16,16,64]{2,0,1:T(8,128)(2,1)S(1)} fusion(bf16[6144,16,64]{0,2,1:T(8,128)(2,1)} %param.14, bf16[16,6144]{1,0:T(8,128)(2,1)S(1)} %copy-done.3), kind=kOutput, calls=%fused_computation.18 | convolution fusion | flops 201326592 | bytes 12812288 | tf_op jit(solution)/shard_map/bd,dhr->bhr/dot_general | solution.py:20
  27.7 8.8 %all_gather.7 = bf16[16,64,64]{2,1,0:T(8,128)(2,1)S(1)} all-gather(bf16[16,16,64]{2,1,0:T(8,128)(2,1)S(1)} %copy.30), channel_id=1, replica_groups=mesh['batch'=2,'ctx'=4,'seq'=4] {'seq'}, dimensions={1}, use_global_device_ids=true | all-gather | bytes 163840 | tf_op jit(solution)/shard_map/all_gather | solution.py:23
  36.5 0.1 broadcast_compare_fusion
  36.6 1.8 fusion.20
  38.4 2.0 all-gather.2.cloned.1.call-done
  40.4 7.0 %fusion.19 = (f32[16,64]{1,0:T(8,128)S(1)}, f32[16,64,512]{2,1,0:T(8,128)S(1)}) fusion(f32[16,64,512]{2,1,0:T(8,128)} %fusion.20, bf16[16,64,512]{2,1,0:T(8,128)(2,1)} %all-gather.2.cloned.1.call-done, bf16[16,512,512]{2,1,0:T(8,128)(2,1)} %param.11, pred[16,512]{1,0:T(8,128)(4,1)S(1)} %broadcast_compare_fusion), kind=kOutput, calls=%fused_computation.30 | convolution fusion | flops 538967040 | bytes 13643776 | tf_op jit(solution)/shard_map/bhc,btc->bht/dot_general | solution.py:24
  47.4 33.1 %pmax.7 = f32[16,64]{1,0:T(8,128)S(1)} all-reduce(f32[16,64]{1,0:T(8,128)S(1)} %get-tuple-element.7), channel_id=1, replica_groups=mesh['batch'=2,'ctx'=4,'seq'=4] {'ctx','seq'}, use_global_device_ids=true, to_apply=%region_1.2 | all-reduce | flops 1024 | bytes 8192 | tf_op jit(solution)/shard_map/pmax | solution.py:34
  80.5 0.6 fusion.2
  81.2 6.5 %convolution_multiply_fusion = f32[16,64,512]{2,1,0:T(8,128)} fusion(bf16[16,512,512]{2,1,0:T(8,128)(2,1)} %param.11, f32[16,64,512]{2,1,0:T(8,128)S(1)} %get-tuple-element.8, f32[16,64]{1,0:T(8,128)S(1)} %get-tuple-element.6, f32[16,64]{1,0:T(8,128)S(1)} %get-tuple-element.7, pred[16,512]{1,0:T(8,128)(4,1)S(1)} %broadcast_compare_fusion), kind=kOutput, calls=%fused_computation.7 | convolution fusion | flops 538968064 | bytes 12599296 | tf_op jit(solution)/shard_map/bht,btc->bhc/dot_general | solution.py:33
  87.7 0.0 reduce-scatter.5.cloned.1.call-update
  87.7 0.0 reduce-scatter.7.cloned.1.call-start
  87.7 0.7 copy.16
  88.4 0.0 reduce-scatter.7.cloned.1.call-update
  88.5 0.0 all-reduce.3.cloned.1.call-start
  88.5 27.6 %reduce-scatter.5.cloned.1.call-done = f32[16,16,512]{2,1,0:T(8,128)} async-done(((f32[16,64,512]{2,1,0:T(8,128)}), f32[16,16,512]{2,1,0:T(8,128)}) %reduce-scatter.5.cloned.1.call-update) | async-done | bytes 524304 | tf_op jit(solution)/shard_map/reduce_scatter | solution.py:36
  116.1 0.0 all-reduce.3.cloned.1.call-update
  116.2 0.0 all-reduce.5.cloned.1.call-start
  116.2 21.9 %reduce-scatter.7.cloned.1.call-done = f32[16,16]{1,0:T(8,128)} async-done(((f32[64,16]{1,0:T(8,128)}), f32[16,16]{1,0:T(8,128)}) %reduce-scatter.7.cloned.1.call-update) | async-done | bytes 1040
  138.1 0.8 copy.17
  138.9 12.0 %psum.22 = f32[16,16]{1,0:T(8,128)S(1)} all-reduce(f32[16,16]{1,0:T(8,128)S(1)} %copy.17), channel_id=1, replica_groups=mesh['batch'=2,'ctx'=4,'seq'=4] {'ctx'}, use_global_device_ids=true, to_apply=%region_6.7 | all-reduce | flops 256 | bytes 2048 | tf_op jit(solution)/shard_map/psum | solution.py:39
  150.9 28.4 %all-reduce.3.cloned.1.call-done = f32[16,16,512]{2,1,0:T(8,128)} async-done(((f32[16,16,512]{2,1,0:T(8,128)}), f32[16,16,512]{2,1,0:T(8,128)}) %all-reduce.3.cloned.1.call-update) | async-done | bytes 524304 | tf_op jit(solution)/shard_map/psum | solution.py:38
  179.3 1.1 divide_convert_fusion
  180.5 11.7 %convolution_bitcast_fusion = f32[16,6144]{1,0:T(8,128)} fusion(bf16[16,128,6144]{2,1,0:T(8,128)(2,1)} %param.17, bf16[16,512,128]{2,1,0:T(8,128)(2,1)} %param.16, bf16[16,16,512]{2,1,0:T(8,128)(2,1)S(1)} %divide_convert_fusion), kind=kOutput, calls=%fused_computation.2 | convolution fusion | flops 436240384 | bytes 27918336 | tf_op jit(solution)/shard_map/bhv,hvd->bd/dot_general | solution.py:42
  192.1 0.0 all-reduce.5.cloned.1.call-update
  192.1 32.5 %all-reduce.5.cloned.1.call-done = f32[16,6144]{1,0:T(8,128)} async-done(((f32[16,6144]{1,0:T(8,128)}), f32[16,6144]{1,0:T(8,128)}) %all-reduce.5.cloned.1.call-update) | async-done | bytes 393232 | tf_op jit(solution)/shard_map/psum | solution.py:43
  224.7 1.7 add_convert_fusion
  (14 shorter events, 0.1 us)
Async XLA Ops:
  6.5 11.7 %copy-start = (bf16[16,128,512]{2,1,0:T(8,128)(2,1)S(1)}, bf16[16,128,512]{2,1,0:T(8,128)(2,1)}, u32[]{:S(2)}) copy-start(bf16[16,128,512]{2,1,0:T(8,128)(2,1)} %param.15) | copy-start | bytes 6291460
  6.5 33.9 %all-gather.2.cloned.1.call-start = ((), (), s32[]{:S(2)}) async-start(), calls=%async_computation.2 | async-start | bytes 1310720 | tf_op jit(solution)/shard_map/all_gather | solution.py:22
  18.3 1.4 copy-start.3
  19.6 96.6 %reduce-scatter.5.cloned.1.call-start = ((), (), s32[]{:S(2)}) async-start(), calls=%async_computation.3 | async-start | bytes 2621440 | tf_op jit(solution)/shard_map/reduce_scatter | solution.py:36
  19.6 16.9 %copy-start.4 = (s32[16]{0:T(128)S(1)}, s32[16]{0:T(128)}, u32[]{:S(2)}) copy-start(s32[16]{0:T(128)} %param.10) | copy-start | bytes 196
  19.7 16.9 %copy-start.2 = (bf16[16,512,64]{1,2,0:T(8,128)(2,1)S(1)}, bf16[16,512,64]{1,2,0:T(8,128)(2,1)}, u32[]{:S(2)}) copy-start(bf16[16,512,64]{1,2,0:T(8,128)(2,1)} %param.12) | copy-start | bytes 3145732
  87.7 50.4 %reduce-scatter.7.cloned.1.call-start = ((), (), s32[]{:S(2)}) async-start(), calls=%async_computation.6 | async-start | bytes 40960
  88.5 90.8 %all-reduce.3.cloned.1.call-start = ((), (), s32[]{:S(2)}) async-start(), calls=%async_computation.4 | async-start | bytes 1048576 | tf_op jit(solution)/shard_map/psum | solution.py:38
  116.2 108.5 %all-reduce.5.cloned.1.call-start = ((), (), s32[]{:S(2)}) async-start(), calls=%async_computation.5 | async-start | bytes 786432 | tf_op jit(solution)/shard_map/psum | solution.py:43
  180.4 45.9 %copy-start.1 = (bf16[16,128,512]{2,1,0:T(8,128)(2,1)S(1)}, bf16[16,128,512]{2,1,0:T(8,128)(2,1)}, u32[]{:S(2)}) copy-start(bf16[16,128,512]{2,1,0:T(8,128)(2,1)} %param.15) | copy-start | bytes 6291460
Sparse Core Ops, SparseCore 0:
  19.7 20.6 all-gather.1
  87.8 28.2 reduce-scatter.4
  118.6 19.5 reduce-scatter.6
  140.3 38.9 all-reduce.2
  192.3 32.3 all-reduce.4
where the time goes:
time: 233 us
  waiting for transfers between devices  113 us (48%)
  blocking collectives  53.9 us (23%)
  matrix products  47 us (20%)
  between operations  13.3 us (6%)
  other arithmetic  3.59 us (2%)
  local copies, waits for them, and re-layouts  2.42 us (1%)
    pmax x1, blocking collectives, local_step(): global_max = lax.pmax(local_max, ('ctx', 'seq'))  33.1 us
    psum x1, waiting for transfers between devices, local_step(): mixed = lax.psum(mixed_part, 'seq')  32.5 us
    psum x1, waiting for transfers between devices, local_step(): acc_heads = lax.psum(acc_heads, 'ctx')  28.4 us
    reduce_scatter x1, waiting for transfers between devices, local_step(): lax.psum_scatter(local_acc * rescale[:, :, None], 'seq', scatter_dimensio...  27.6 us
    unnamed x6, waiting for transfers between devices  22 us
    psum x1, blocking collectives, local_step(): sum_heads = lax.psum(sum_heads, 'ctx')  12 us
    dot_general x1, matrix products, local_step(): jnp.einsum('bd,dhk->bhk', hidden, w_uq, preferred_element_type=jnp.float32)  11.7 us
    dot_general x1, matrix products, local_step(): jnp.einsum('bhv,hvd->bd', head_vals, w_out, preferred_element_type=jnp.fl...  11.7 us
  transfers between devices with their start and end apart: 5, of which 5 were waited for; matrix products, arithmetic and copies ran while one was open for 5% of the time, Pallas kernels for 0%

commit v1 on v0

v1 whole, which is shorter than its diff:
```python
import functools

import jax
import jax.numpy as jnp
from jax import lax
from jax.experimental import pallas as pl
from jax.experimental.pallas import tpu as pltpu
from jax.sharding import PartitionSpec as P

MESH = pl.DeviceIdType.MESH
F32, BF16 = jnp.float32, jnp.bfloat16
NEG = -3.0e38

ROWS, D, HLOC, NOPE, ROPE, LAT, VAL = 16, 6144, 16, 128, 64, 512, 128
TLOC = 512
QW = LAT + 128
CH = 768
NCH = D // CH
SLOTS = 4
HALF = D // 2


def mm(a, b):
    return lax.dot_general(a, b, (((1,), (0,)), ((), ())), preferred_element_type=F32)


def mm_nt(a, b):
    return lax.dot_general(a, b, (((1,), (1,)), ((), ())), preferred_element_type=F32)


def onehot(shape, fn):
    i = lax.broadcasted_iota(jnp.int32, shape, 0)
    j = lax.broadcasted_iota(jnp.int32, shape, 1)
    return jnp.where(fn(i, j), 1.0, 0.0).astype(BF16)


def merge(a, mla, b, mlb):
    ma, mb = mla[:, 0:1], mlb[:, 0:1]
    m = jnp.maximum(ma, mb)
    fa, fb = jnp.exp(ma - m), jnp.exp(mb - m)
    l = mla[:, 1:2] * fa + mlb[:, 1:2] * fb
    return a * fa + b * fb, pack_ml(m, l)


def pack_ml(m, l):
    lane = lax.broadcasted_iota(jnp.int32, (m.shape[0], 128), 1)
    return jnp.where(lane == 0, m, jnp.where(lane == 1, l, 0.0))


def kernel(len_ref, hid_hbm, cache_hbm, rope_hbm, wuq_hbm, wqr_hbm, wuk_hbm, wuv_hbm, wout_hbm, out_ref,
           hid, cache, rope, wuq, wqr, wuk, wuv, wout, rep, qall, qb, acc, ml, racc, rml, ysa, ysm, yra, yrm,
           zsa, zsm, zra, zrm, yb, yr, tr, fin, hsel, outf,
           lsem, usem, csem, bar_unused, ag_s, ag_r, d_s, d_r, y_s, y_r, z_s, z_r, f_s, f_r):
    x = lax.axis_index("batch")
    z = lax.axis_index("ctx")
    s = lax.axis_index("seq")
    y, k = s // 2, s % 2
    sp = s + 1 - 2 * k
    sy = s + 2 - 4 * y
    zx = {1: z + 1 - 2 * (z % 2), 2: z + 2 - 4 * (z // 2), 3: 3 - z}

    dev_p, dev_y = (x, z, sp), (x, z, sy)
    dev_z = {j: (x, zx[j], s) for j in zx}
    peers = [dev_p, dev_y, dev_z[1], dev_z[2], dev_z[3]]

    barrier = pltpu.get_barrier_semaphore()
    for d in peers:
        pl.semaphore_signal(barrier, inc=1, device_id=d, device_id_type=MESH)

    def local(src, dst, sem):
        c = pltpu.make_async_copy(src, dst, sem)
        c.start()
        return c

    def remote(src, dst, ss, rs, dev):
        return pltpu.make_async_remote_copy(src_ref=src, dst_ref=dst, send_sem=ss, recv_sem=rs,
                                            device_id=dev, device_id_type=MESH)

    c_hid = local(hid_hbm, hid, lsem.at[0])
    hh = pl.multiple_of(8 * (z // 2), 8)

    def uq_copy(i, slot):
        return pltpu.make_async_copy(wuq_hbm.at[pl.ds(pl.multiple_of(i * CH, CH), CH), pl.ds(hh, 8), :],
                                     wuq.at[slot], usem.at[slot])

    for i in range(SLOTS):
        uq_copy(i, i).start()
    c_qr = local(wqr_hbm.at[pl.ds(4 * z, 4)], wqr, lsem.at[1])
    c_uk = local(wuk_hbm.at[pl.ds(4 * z, 4)], wuk, lsem.at[2])

    spread = onehot((128, 1024), lambda i, j: j // 8 == i)
    c_hid.wait()

    for t in range(6):
        blk = jnp.concatenate([hid[:, (8 * t + i) * 128:(8 * t + i + 1) * 128] for i in range(8)], axis=0)
        rep[pl.ds(8 * t, 8)] = mm(blk, spread).astype(BF16).reshape(8, 16, 1024)

    lane = lax.broadcasted_iota(jnp.int32, (16, 128), 1)
    masks = [jnp.where(lane % 8 == 4 * (z % 2) + h, 1.0, 0.0).astype(BF16) for h in range(4)]
    wide = [jnp.concatenate([m] * (CH * 8 // 128), axis=1) for m in masks]

    def chunk(i, qn):
        slot = lax.rem(i, SLOTS)
        uq_copy(i, slot).wait()
        r = jnp.concatenate([rep[i * 6 + t] for t in range(6)], axis=1)
        lhs = jnp.concatenate([r * m for m in wide], axis=0)
        qn = qn + mm(lhs, wuq[slot].reshape(CH * 8, NOPE))

        @pl.when(i + SLOTS < NCH)
        def _():
            uq_copy(i + SLOTS, slot).start()
        return qn

    qn = lax.fori_loop(0, NCH, chunk, jnp.zeros((64, NOPE), F32)).astype(BF16)

    c_rope = local(rope_hbm, rope, lsem.at[3])
    c_cache = [local(cache_hbm.at[pl.ds(4 * g, 4)], cache.at[pl.ds(4 * g, 4)], csem.at[g]) for g in range(4)]
    c_uv = local(wuv_hbm, wuv, lsem.at[4])
    c_out = local(wout_hbm, wout, lsem.at[5])

    c_qr.wait()
    qr = mm_nt(hid[...], wqr[...].reshape(4 * ROPE, D)).astype(BF16)
    c_uk.wait()
    parts = []
    for h in range(4):
        ql = mm(qn[16 * h:16 * h + 16], wuk[h]).astype(BF16)
        rr = jnp.concatenate([qr[:, ROPE * h:ROPE * h + ROPE], jnp.zeros((16, 64), BF16)], axis=1)
        parts.append(jnp.concatenate([ql, rr], axis=1))
    q = jnp.concatenate(parts, axis=0)
    turn = onehot((64, 64), lambda i, j: (i % 4) * 16 + i // 4 == j)
    me = s * 4 + z
    qall[me] = mm(turn, q).astype(BF16)

    pl.semaphore_wait(barrier, len(peers))
    sends = []

    def send(piece, sem_i, dev):
        c = remote(qall.at[piece], qall.at[piece], ag_s.at[sem_i], ag_r.at[piece], dev)
        c.start()
        sends.append(c)

    def arrived(piece):
        remote(qall.at[piece], qall.at[piece], ag_s.at[0], ag_r.at[piece], dev_p).wait_recv()

    send(me, 0, dev_y)
    for n, j in enumerate((1, 2, 3)):
        send(me, 1 + n, dev_z[j])
    send(me, 4, dev_p)
    ns = 5
    for j in (1, 2, 3):
        pz = s * 4 + zx[j]
        arrived(pz)
        send(pz, ns, dev_y)
        send(pz, ns + 1, dev_p)
        ns += 2
    for zz in (z, zx[1], zx[2], zx[3]):
        py = sy * 4 + zz
        arrived(py)
        send(py, ns, dev_p)
        ns += 1

    pick = onehot((16, 16), lambda i, j: 4 * z + i == j)
    hsel[...] = mm(pick, hid[...])[0:4]

    for ss in (sp, sp + 2 - 4 * y):
        for zz in (z, zx[1], zx[2], zx[3]):
            arrived(ss * 4 + zz)
    for c in sends:
        c.wait_send()

    perm = onehot((256, 256), lambda i, j: ((i % 64) // 4) * 16 + (i // 64) * 4 + i % 4 == j)
    scale = (NOPE + ROPE) ** -0.5
    t0 = (z * 4 + s) * TLOC
    c_rope.wait()
    for c in c_cache:
        c.wait()

    def attend(g):
        rows = pl.ds(pl.multiple_of(16 * g, 16), 16)
        xg = jnp.concatenate([qall[p, rows, :] for p in range(16)], axis=0)
        qb[...] = mm(perm, xg).astype(BF16).reshape(4, 64, QW)

        def row(i, carry):
            b = 4 * g + i
            q = qb[i]
            kv = cache[b]
            sc = mm_nt(q[:, :LAT], kv) + mm(q[:, LAT:LAT + ROPE], rope[b])
            sc = sc * scale
            valid = lax.broadcasted_iota(jnp.int32, (64, TLOC), 1) < len_ref[b] - t0
            sc = jnp.where(valid, sc, NEG)
            m = jnp.max(sc, axis=1, keepdims=True)
            w = jnp.where(valid, jnp.exp(sc - m), 0.0)
            l = jnp.sum(w, axis=1, keepdims=True)
            acc[b] = mm(w.astype(BF16), kv).reshape(4, 16, LAT)
            ml[b] = pack_ml(m, l).reshape(4, 16, 128)
            return carry

        lax.fori_loop(0, 4, row, 0)

    def d_copies(j, g):
        out = []
        for n in range(2):
            so = 2 * n + (1 - k)
            rows = pl.ds(4 * g, 4)
            out.append(remote(acc.at[rows, so], racc.at[j, n], d_s.at[j, 2 * n], d_r.at[j, 2 * n], dev_p))
            out.append(remote(ml.at[rows, so], rml.at[j, n], d_s.at[j, 2 * n + 1], d_r.at[j, 2 * n + 1], dev_p))
        return out

    def y_copies(j):
        return [remote(ysa.at[j], yra.at[j], y_s.at[j, 0], y_r.at[j, 0], dev_y),
                remote(ysm.at[j], yrm.at[j], y_s.at[j, 1], y_r.at[j, 1], dev_y)]

    def z_copies(j):
        return [remote(zsa.at[j], zra.at[j], z_s.at[j, 0], z_r.at[j, 0], dev_z[j]),
                remote(zsm.at[j], zrm.at[j], z_s.at[j, 1], z_r.at[j, 1], dev_z[j])]

    order = (3, 2, 1, 0)
    gs = {0: z, **zx}

    def stage_d(j):
        attend(gs[j])
        for c in d_copies(j, gs[j]):
            c.start()

    def stage_y(j):
        for c in d_copies(j, gs[j]):
            c.wait_recv()
        for n in range(2):
            so = 2 * n + k

            def piece(i, carry):
                b = 4 * gs[j] + i
                a, q = merge(acc[b, so], ml[b, so], racc[j, n, i], rml[j, n, i])
                acc[b, so] = a
                ml[b, so] = q
                return carry
            lax.fori_loop(0, 4, piece, 0)

        def give(i, carry):
            ysa[j, i] = acc[4 * gs[j] + i, 2 * (1 - y) + k]
            ysm[j, i] = ml[4 * gs[j] + i, 2 * (1 - y) + k]
            return carry
        lax.fori_loop(0, 4, give, 0)
        for c in y_copies(j):
            c.start()

    def stage_z(j):
        for c in y_copies(j):
            c.wait_recv()

        def piece(i, carry):
            b = 4 * gs[j] + i
            a, q = merge(acc[b, s], ml[b, s], yra[j, i], yrm[j, i])
            zsa[j, i] = a
            zsm[j, i] = q
            return carry
        lax.fori_loop(0, 4, piece, 0)
        if j:
            for c in z_copies(j):
                c.start()

    for n in range(len(order) + 2):
        if n < 4:
            stage_d(order[n])
        if 0 <= n - 1 < 4:
            stage_y(order[n - 1])
        if 0 <= n - 2 < 4:
            stage_z(order[n - 2])

    for j in (1, 2, 3):
        for c in z_copies(j):
            c.wait_recv()
    ol = []
    for i in range(4):
        a, q = zsa[0, i], zsm[0, i]
        for j in (1, 2, 3):
            a, q = merge(a, q, zra[j, i], zrm[j, i])
        ol.append((a / q[:, 1:2]).astype(BF16))
    ol = jnp.concatenate(ol, axis=0)

    c_uv.wait()
    vs = []
    head = lax.broadcasted_iota(jnp.int32, (64, VAL), 0) % 16
    for h in range(HLOC):
        v = mm(ol, wuv[h])
        vs.append(jnp.where(head == h, v, 0.0).astype(BF16))
    v = jnp.concatenate(vs, axis=1)
    fold = onehot((16, 64), lambda i, j: j // 16 == i)
    v = mm(fold, v).astype(BF16)

    c_out.wait()
    w = 768
    for n in range(2):
        def cols(i, carry):
            at = pl.multiple_of(n * HALF + i * w, w)
            r = mm(v, wout[:, :, pl.ds(at, w)].reshape(HLOC * VAL, w))
            yb[n, :, pl.ds(pl.multiple_of(i * w, w), w)] = r[0:4]
            return carry
        lax.fori_loop(0, HALF // w, cols, 0)

    c = remote(yb, yr, f_s.at[0], f_r.at[0], dev_p)
    c.start()
    c.wait_recv()
    tr[0] = yb[k] + yr[k]
    cy = remote(tr.at[0], tr.at[1], f_s.at[1], f_r.at[1], dev_y)
    cy.start()
    cy.wait_recv()
    res = hsel[:, pl.ds(pl.multiple_of(k * HALF, HALF), HALF)] + (tr[0] + tr[1])
    fin[z, k] = res.astype(BF16)

    last = [remote(fin.at[z, k], fin.at[z, k], f_s.at[2], f_r.at[2], dev_p)]
    for j in (1, 2, 3):
        last.append(remote(fin.at[z, k], fin.at[z, k], f_s.at[2 + j], f_r.at[2 + j], dev_z[j]))
    for d in last:
        d.start()
    for j in (1, 2, 3):
        remote(fin.at[zx[j], k], fin.at[zx[j], k], f_s.at[2 + j], f_r.at[2 + j], dev_z[j]).wait_recv()
        d = remote(fin.at[zx[j], k], fin.at[zx[j], k], f_s.at[5 + j], f_r.at[5 + j], dev_p)
        d.start()
        last.append(d)
    remote(fin.at[z, 1 - k], fin.at[z, 1 - k], f_s.at[2], f_r.at[2], dev_p).wait_recv()
    for j in (1, 2, 3):
        remote(fin.at[zx[j], 1 - k], fin.at[zx[j], 1 - k], f_s.at[5 + j], f_r.at[5 + j], dev_p).wait_recv()
    for i in range(4):
        for n in range(2):
            outf[4 * i:4 * i + 4, n * HALF:(n + 1) * HALF] = fin[i, n].astype(F32)
    out_ref[...] = outf[...].astype(BF16)

    for j in order:
        for d in d_copies(j, gs[j]) + y_copies(j) + (z_copies(j) if j else []):
            d.wait_send()
    for d in [c, cy] + last:
        d.wait_send()


def solution(mesh):
    def local_step(hidden, lengths, latent_cache, rope_keys, w_uq, w_qr, w_uk, w_uv, w_out):
        rope_t = jnp.transpose(rope_keys, (0, 2, 1))
        wqr_t = jnp.transpose(w_qr, (1, 2, 0))
        anyspec = pl.BlockSpec(memory_space=pl.ANY)
        dma = pltpu.SemaphoreType.DMA
        scratch = [
            pltpu.VMEM((ROWS, D), BF16),
            pltpu.VMEM((ROWS, TLOC, LAT), BF16),
            pltpu.VMEM((ROWS, ROPE, TLOC), BF16),
            pltpu.VMEM((SLOTS, CH, 8, NOPE), BF16),
            pltpu.VMEM((4, ROPE, D), BF16),
            pltpu.VMEM((4, NOPE, LAT), BF16),
            pltpu.VMEM((HLOC, LAT, VAL), BF16),
            pltpu.VMEM((HLOC, VAL, D), BF16),
            pltpu.VMEM((48, 16, 1024), BF16),
            pltpu.VMEM((16, 64, QW), BF16),
            pltpu.VMEM((4, 64, QW), BF16),
            pltpu.VMEM((ROWS, 4, 16, LAT), F32),
            pltpu.VMEM((ROWS, 4, 16, 128), F32),
            pltpu.VMEM((4, 2, 4, 16, LAT), F32),
            pltpu.VMEM((4, 2, 4, 16, 128), F32),
            pltpu.VMEM((4, 4, 16, LAT), F32),
            pltpu.VMEM((4, 4, 16, 128), F32),
            pltpu.VMEM((4, 4, 16, LAT), F32),
            pltpu.VMEM((4, 4, 16, 128), F32),
            pltpu.VMEM((4, 4, 16, LAT), F32),
            pltpu.VMEM((4, 4, 16, 128), F32),
            pltpu.VMEM((4, 4, 16, LAT), F32),
            pltpu.VMEM((4, 4, 16, 128), F32),
            pltpu.VMEM((2, 4, HALF), F32),
            pltpu.VMEM((2, 4, HALF), F32),
            pltpu.VMEM((2, 4, HALF), F32),
            pltpu.VMEM((4, 2, 4, HALF), BF16),
            pltpu.VMEM((4, D), F32),
            pltpu.VMEM((ROWS, D), F32),
            dma((6,)), dma((SLOTS,)), dma((4,)), dma((1,)),
            dma((15,)), dma((16,)),
            dma((4, 4)), dma((4, 4)),
            dma((4, 2)), dma((4, 2)),
            dma((4, 2)), dma((4, 2)),
            dma((9,)), dma((9,)),
        ]
        return pl.pallas_call(
            kernel,
            out_shape=jax.ShapeDtypeStruct((ROWS, D), BF16),
            in_specs=[pl.BlockSpec(memory_space=pltpu.SMEM)] + [anyspec] * 8,
            out_specs=pl.BlockSpec(memory_space=pltpu.VMEM),
            scratch_shapes=scratch,
            compiler_params=pltpu.CompilerParams(collective_id=0, has_side_effects=True,
                                                 vmem_limit_bytes=67_000_000),
        )(lengths, hidden, latent_cache, rope_t, w_uq, wqr_t, w_uk, w_uv, w_out)

    row_spec, cache_spec = P('batch', None), P('batch', ('ctx', 'seq'), None)
    head_spec, proj_spec = P('seq', None, None), P(None, 'seq', None)
    return jax.shard_map(local_step, mesh=mesh,
                         in_specs=(row_spec, P('batch'), cache_spec, cache_spec, proj_spec, proj_spec, head_spec, head_spec, head_spec),
                         out_specs=row_spec, check_vma=False)
```

time: 233 us -> 73 us (0.31)
  waiting for transfers between devices: 113 us -> 0 us
  Pallas kernels: 0 us -> 71.2 us
  blocking collectives: 53.9 us -> 0 us
  matrix products: 47 us -> 0 us
  between operations: 13.3 us -> 0.01 us
  other arithmetic: 3.59 us -> 0 us
    pallas_call x0 -> x1, Pallas kernels: none -> 71.2 us  [local_step(): pl.pallas_call(kernel, out_shape=jax.ShapeDtypeStruct((ROWS, D), BF16), i...]
    psum x2 -> x0, waiting for transfers between devices: 60.9 us -> none  [the longest x1 32.5 us: local_step(): mixed = lax.psum(mixed_part, 'seq')]
    dot_general x7 -> x0, matrix products: 47 us -> none  [the longest x1 11.7 us: local_step(): jnp.einsum('bd,dhk->bhk', hidden, w_uq, preferred_element_type=jnp.float32)]
    pmax x1 -> x0, blocking collectives: 33.1 us -> none  [local_step(): global_max = lax.pmax(local_max, ('ctx', 'seq'))]
    reduce_scatter x1 -> x0, waiting for transfers between devices: 27.6 us -> none  [local_step(): lax.psum_scatter(local_acc * rescale[:, :, None], 'seq', scatter_dimensio...]
    unnamed x6 -> x0, waiting for transfers between devices: 22 us -> none
    psum x1 -> x0, blocking collectives: 12 us -> none  [local_step(): sum_heads = lax.psum(sum_heads, 'ctx')]
    all_gather x1 -> x0, blocking collectives: 8.83 us -> none  [local_step(): rope_all = lax.all_gather(q_rope, 'seq', axis=1, tiled=True)]
  transfers between devices with their start and end apart: 5 -> 0, of which waited for: 5 -> 0; matrix products, arithmetic and copies ran while one was open for 5% -> 0% of each run, Pallas kernels for 0% -> 0%
where the time goes in v1:
time: 73 us; the launch traced here: 72.8 us
  Pallas kernels  71.2 us (98%)
  local copies, waits for them, and re-layouts  1.62 us (2%)
    pallas_call x1, Pallas kernels, local_step(): pl.pallas_call(kernel, out_shape=jax.ShapeDtypeStruct((ROWS, D), BF16), i...  71.2 us
    unnamed x1, local copies, waits for them, and re-layouts  1.62 us

profile of v1, /device:TPU:0, one launch (start us, length us, event | category | flops | bytes accessed | tf_op | source)
XLA Modules:
  0.0 72.8 jit_solution(5121530200578359115)
XLA Ops:
  0.0 71.2 %shard_map.91 = bf16[16,6144]{1,0:T(8,128)(2,1)} custom-call(s32[16]{0:T(128)} %len_ref.1, bf16[16,6144]{1,0:T(8,128)(2,1)} %hid_hbm.1, bf16[16,512,512]{2,1,0:T(8,128)(2,1)} %cache_hbm.1, bf16[16,64,512]{2,1,0:T(8,128)(2,1)} %bitcast.3, bf16[6144,16,128]{2,1,0:T(8,128)(2,1)} %wuq_hbm.1, bf16[16,64,6144]{2,1,0:T(8,128)(2,1)} %bitcast.2, ...), custom_call_target="tpu_custom_call" | custom-call | tf_op jit(solution)/shard_map/pallas_call | solution.py:379
  71.2 1.6 %copy.11 = bf16[16,6144]{1,0:T(8,128)(2,1)} copy(bf16[16,6144]{1,0:T(8,128)(2,1)} %shard_map.91) | data formatting | bytes 393216

commit v2 on v0

v2 whole, which is shorter than its diff:
```python
import functools

import jax
import jax.numpy as jnp
from jax import lax
from jax.experimental import pallas as pl
from jax.experimental.pallas import tpu as pltpu
from jax.sharding import PartitionSpec as P

MESH = pl.DeviceIdType.MESH
F32, BF16 = jnp.float32, jnp.bfloat16
NEG = -3.0e38

ROWS, D, HLOC, NOPE, ROPE, LAT, VAL = 16, 6144, 16, 128, 64, 512, 128
TLOC = 512
QW = LAT + 128
CH = 1536
NCH = D // CH
BLK = CH // 128
QUART = D // 4


def mm(a, b):
    return lax.dot_general(a, b, (((1,), (0,)), ((), ())), preferred_element_type=F32)


def mm_nt(a, b):
    return lax.dot_general(a, b, (((1,), (1,)), ((), ())), preferred_element_type=F32)


def onehot(shape, fn):
    i = lax.broadcasted_iota(jnp.int32, shape, 0)
    j = lax.broadcasted_iota(jnp.int32, shape, 1)
    return jnp.where(fn(i, j), 1.0, 0.0).astype(BF16)


def put(ml, i, m, l):
    lane = lax.broadcasted_iota(jnp.int32, ml.shape, 1)
    return jnp.where(lane == i, m, jnp.where(lane == 4 + i, l, ml))


def merge4(parts, mls):
    out, ml = [], jnp.zeros((16, 128), F32)
    for i in range(4):
        ms = [q[:, i:i + 1] for q in mls]
        m = functools.reduce(jnp.maximum, ms)
        fs = [jnp.exp(v - m) for v in ms]
        l = functools.reduce(jnp.add, [q[:, 4 + i:5 + i] * f for q, f in zip(mls, fs)])
        out.append(functools.reduce(jnp.add, [p(i) * f for p, f in zip(parts, fs)]))
        ml = put(ml, i, m, l)
    return out, ml


def kernel(len_ref, hid_hbm, cache_hbm, rope_hbm, wuq_hbm, wqr_hbm, wuk_hbm, wuv_hbm, wout_hbm, out_ref,
           hid, cache, rope, wuq, wqr, wuk, wuv, wout, rep, zq, qnb, qg, acc, ml, racc, rml,
           yra, yrm, zra, zrm, yb, yr, tr, fin, hsel, outf,
           lsem, usem, csem, q_s, q_r, a_s, a_r, d_s, d_r, y_s, y_r, z_s, z_r, e_s, e_r, t_s, t_r, f_s, f_r):
    x = lax.axis_index("batch")
    z = lax.axis_index("ctx")
    s = lax.axis_index("seq")
    y, k = s // 2, s % 2
    sp = s + 1 - 2 * k
    sy = s + 2 - 4 * y
    spy = sp + 2 - 4 * y
    zx = {1: z + 1 - 2 * (z % 2), 2: z + 2 - 4 * (z // 2), 3: 3 - z}
    gs = {0: z, **zx}
    order = (3, 2, 1, 0)

    dev_p, dev_y = (x, z, sp), (x, z, sy)
    dev_z = {j: (x, zx[j], s) for j in zx}
    peers = [dev_p, dev_y, dev_z[1], dev_z[2], dev_z[3]]

    barrier = pltpu.get_barrier_semaphore()
    for d in peers:
        pl.semaphore_signal(barrier, inc=1, device_id=d, device_id_type=MESH)

    def local(src, dst, sem):
        c = pltpu.make_async_copy(src, dst, sem)
        c.start()
        return c

    def remote(src, dst, ss, rs, dev):
        return pltpu.make_async_remote_copy(src_ref=src, dst_ref=dst, send_sem=ss, recv_sem=rs,
                                            device_id=dev, device_id_type=MESH)

    started = []

    def go(c):
        c.start()
        started.append(c)

    own4 = pl.ds(pl.multiple_of(4 * z, 4), 4)
    c_hid = local(hid_hbm, hid, lsem.at[0])

    def load_uq(i):
        return local(wuq_hbm.at[pl.ds(i * CH, CH), own4, :], wuq.at[i], usem.at[i])

    c_uq = [load_uq(0), load_uq(1)]
    c_qr = local(wqr_hbm.at[own4], wqr, lsem.at[1])
    c_uq += [load_uq(2), load_uq(3)]
    c_uk = local(wuk_hbm, wuk, lsem.at[2])

    spread = onehot((128, 512), lambda i, j: j // 4 == i)
    lane = lax.broadcasted_iota(jnp.int32, (16, 128), 1)
    masks = [jnp.where(lane % 4 == h, 1.0, 0.0).astype(BF16) for h in range(4)]
    wide = [jnp.concatenate([m] * (CH * 4 // 128), axis=1) for m in masks]
    c_hid.wait()
    for t in range(NCH):
        blk = jnp.concatenate([hid[:, (BLK * t + i) * 128:(BLK * t + i + 1) * 128] for i in range(BLK)], axis=0)
        rep[pl.ds(BLK * t, BLK)] = mm(blk, spread).astype(BF16).reshape(BLK, 16, 512)
    qn = jnp.zeros((64, NOPE), F32)
    for i in range(NCH):
        c_uq[i].wait()
        r = jnp.concatenate([rep[i * BLK + t] for t in range(BLK)], axis=1)
        lhs = jnp.concatenate([r * m for m in wide], axis=0)
        qn = qn + mm(lhs, wuq[i].reshape(CH * 4, NOPE))
        if i == 1:
            c_qr.wait()
            qr = mm_nt(hid[...], wqr[...].reshape(4 * ROPE, D)).astype(BF16)
    qn = qn.astype(BF16)
    rr = jnp.concatenate([qr[:, ROPE * h:ROPE * h + ROPE] for h in range(4)], axis=0)
    zq[z] = jnp.concatenate([qn, rr, jnp.zeros((64, 64), BF16)], axis=1)
    c_rope = local(rope_hbm, rope, lsem.at[3])
    c_cache = {j: local(cache_hbm.at[pl.ds(4 * gs[j], 4)], cache.at[pl.ds(4 * gs[j], 4)], csem.at[j]) for j in order}
    c_uv = local(wuv_hbm, wuv, lsem.at[4])
    c_out = local(wout_hbm, wout, lsem.at[5])

    pl.semaphore_wait(barrier, len(peers))
    for j in (3, 2, 1):
        go(remote(zq.at[z], zq.at[z], q_s.at[j - 1], q_r.at[z], dev_z[j]))
    pick = onehot((16, 16), lambda i, j: 4 * z + i == j)
    hsel[...] = mm(pick, hid[...])[0:4]
    perm = onehot((256, 256), lambda i, j: (i % 16) * 16 + i // 16 == j)
    row16 = lax.broadcasted_iota(jnp.int32, (16, 128), 0)
    hm = [jnp.concatenate([jnp.where(row16 == h, 1.0, 0.0).astype(BF16)] * 4, axis=0) for h in range(HLOC)]
    for j in (1, 2, 3):
        remote(zq.at[zx[j]], zq.at[zx[j]], q_s.at[0], q_r.at[zx[j]], dev_p).wait_recv()
    qnb[...] = mm(perm, zq[...].reshape(256, 256)).astype(BF16).reshape(4, 64, 256)
    c_uk.wait()

    for j in order:
        qb = qnb[gs[j]]
        lhs = jnp.concatenate([qb[:, :NOPE] * hm[h] for h in range(HLOC)], axis=1)
        ql = mm(lhs, wuk[...].reshape(HLOC * NOPE, LAT)).astype(BF16)
        qg[j, s] = jnp.concatenate([ql, qb[:, NOPE:]], axis=1)
        go(remote(qg.at[j, s], qg.at[j, s], a_s.at[j, 0], a_r.at[j, s], dev_y))
        go(remote(qg.at[j, s], qg.at[j, s], a_s.at[j, 1], a_r.at[j, s], dev_p))

    def arrived(j, who):
        remote(qg.at[j, who], qg.at[j, who], a_s.at[j, 0], a_r.at[j, who], dev_p).wait_recv()

    def forward(j):
        arrived(j, sy)
        go(remote(qg.at[j, sy], qg.at[j, sy], a_s.at[j, 2], a_r.at[j, sy], dev_p))

    scale = (NOPE + ROPE) ** -0.5
    t0 = (z * 4 + s) * TLOC

    def attend(j, rows, mlv):
        sc, ws = [], []
        for i in rows:
            b = 4 * gs[j] + i
            q = jnp.concatenate([qg[j, p, 16 * i:16 * i + 16, :] for p in range(4)], axis=0)
            sc.append(mm_nt(q[:, :LAT], cache[b]) + mm(q[:, LAT:LAT + ROPE], rope[b]))
        for n, i in enumerate(rows):
            b = 4 * gs[j] + i
            valid = lax.broadcasted_iota(jnp.int32, (64, TLOC), 1) < len_ref[b] - t0
            v = jnp.where(valid, sc[n] * scale, NEG)
            m = jnp.max(v, axis=1, keepdims=True)
            w = jnp.where(valid, jnp.exp(v - m), 0.0)
            mlv = put(mlv, i, m, jnp.sum(w, axis=1, keepdims=True))
            ws.append(w.astype(BF16))
        for n, i in enumerate(rows):
            o = mm(ws[n], cache[4 * gs[j] + i])
            for p in range(4):
                acc[j, p, i] = o[16 * p:16 * p + 16]
        return mlv

    def d_copies(j):
        out = []
        for n in range(2):
            so = 2 * n + (1 - k)
            out.append(remote(acc.at[j, so], racc.at[j, n], d_s.at[j, 2 * n], d_r.at[j, 2 * n], dev_p))
            out.append(remote(ml.at[j, so], rml.at[j, n], d_s.at[j, 2 * n + 1], d_r.at[j, 2 * n + 1], dev_p))
        return out

    def y_copies(j):
        so = 2 * (1 - y) + k
        return [remote(acc.at[j, so], yra.at[j], y_s.at[j, 0], y_r.at[j, 0], dev_y),
                remote(ml.at[j, so], yrm.at[j], y_s.at[j, 1], y_r.at[j, 1], dev_y)]

    def z_copies(j):
        return [remote(acc.at[j, s], zra.at[j], z_s.at[j, 0], z_r.at[j, 0], dev_z[j]),
                remote(ml.at[j, s], zrm.at[j], z_s.at[j, 1], z_r.at[j, 1], dev_z[j])]

    def add(j, so, ra, rm):
        out, q = merge4([lambda i: acc[j, so, i], ra], [ml[j, so], rm])
        for i in range(4):
            acc[j, so, i] = out[i]
        ml[j, so] = q

    def stage_y(j):
        for c in d_copies(j):
            c.wait_recv()
        add(j, 2 * (1 - y) + k, lambda i: racc[j, 1 - y, i], rml[j, 1 - y])
        for c in y_copies(j):
            go(c)
        add(j, s, lambda i: racc[j, y, i], rml[j, y])

    def stage_z(j):
        for c in y_copies(j):
            c.wait_recv()
        add(j, s, lambda i: yra[j, i], yrm[j])
        if j:
            for c in z_copies(j):
                go(c)

    forward(order[0])
    c_rope.wait()
    for n in range(len(order) + 2):
        if n < 4:
            j = order[n]
            arrived(j, sp)
            arrived(j, spy)
            c_cache[j].wait()
            mlv = attend(j, (0, 1), jnp.zeros((64, 128), F32))
            if n < 3:
                forward(order[n + 1])
            mlv = attend(j, (2, 3), mlv)
            ml[j] = mlv.reshape(4, 16, 128)
            for c in d_copies(j):
                go(c)
        if 0 <= n - 1 < 4:
            stage_y(order[n - 1])
        if 0 <= n - 2 < 4:
            stage_z(order[n - 2])

    for j in (1, 2, 3):
        for c in z_copies(j):
            c.wait_recv()
    c_uv.wait()
    c_out.wait()
    out, q = merge4([lambda i: acc[0, s, i]] + [functools.partial(lambda j, i: zra[j, i], j) for j in (1, 2, 3)],
                    [ml[0, s], zrm[1], zrm[2], zrm[3]])
    ol = jnp.concatenate([(out[i] / q[:, 4 + i:5 + i]).astype(BF16) for i in range(4)], axis=0)
    vs = []
    head = lax.broadcasted_iota(jnp.int32, (64, VAL), 0) % 16
    for h in range(HLOC):
        vs.append(jnp.where(head == h, mm(ol, wuv[h]), 0.0).astype(BF16))
    v = jnp.concatenate(vs, axis=1)
    fold = onehot((16, 64), lambda i, j: j // 16 == i)
    v = mm(fold, v).astype(BF16)

    def cols(c):
        at = pl.multiple_of(c * QUART, QUART)
        return mm(v, wout[:, :, pl.ds(at, QUART)].reshape(HLOC * VAL, QUART))[0:4]

    def e_copy(n):
        return remote(yb.at[n], yr.at[n], e_s.at[n], e_r.at[n], dev_p)

    def t_copy(n):
        return remote(tr.at[0, n], tr.at[1, n], t_s.at[n], t_r.at[n], dev_y)

    def finish(n):
        t_copy(n).wait_recv()
        c = 2 * k + n
        res = hsel[:, pl.ds(pl.multiple_of(c * QUART, QUART), QUART)] + (tr[0, n] + tr[1, n])
        fin[z, c] = res.astype(BF16)
        for j in (3, 2, 1):
            go(remote(fin.at[z, c], fin.at[z, c], f_s.at[n, j], f_r.at[n, j], dev_z[j]))
        go(remote(fin.at[z, c], fin.at[z, c], f_s.at[n, 0], f_r.at[n, 0], dev_p))

    for n in range(2):
        yb[n] = cols(2 * (1 - k) + n)
        go(e_copy(n))
    for n in range(2):
        part = cols(2 * k + n)
        e_copy(n).wait_recv()
        tr[0, n] = part + yr[n]
        go(t_copy(n))
        if n:
            finish(0)
    finish(1)
    for n in range(2):
        for j in (1, 2, 3):
            at = fin.at[zx[j], 2 * k + n]
            remote(at, at, f_s.at[n, 0], f_r.at[n, j], dev_p).wait_recv()
            go(remote(at, at, f_s.at[n, 3 + j], f_r.at[n, 3 + j], dev_p))
    for n in range(2):
        for j in range(4):
            at = fin.at[gs[j], 2 * (1 - k) + n]
            remote(at, at, f_s.at[n, 0], f_r.at[n, 3 + j if j else 0], dev_p).wait_recv()
    for i in range(4):
        for c in range(4):
            outf[4 * i:4 * i + 4, c * QUART:(c + 1) * QUART] = fin[i, c].astype(F32)
    out_ref[...] = outf[...].astype(BF16)
    for c in started:
        c.wait_send()


def solution(mesh):
    def local_step(hidden, lengths, latent_cache, rope_keys, w_uq, w_qr, w_uk, w_uv, w_out):
        rope_t = jnp.transpose(rope_keys, (0, 2, 1))
        wqr_t = jnp.transpose(w_qr, (1, 2, 0))
        anyspec = pl.BlockSpec(memory_space=pl.ANY)
        dma = pltpu.SemaphoreType.DMA
        scratch = [
            pltpu.VMEM((ROWS, D), BF16),
            pltpu.VMEM((ROWS, TLOC, LAT), BF16),
            pltpu.VMEM((ROWS, ROPE, TLOC), BF16),
            pltpu.VMEM((NCH, CH, 4, NOPE), BF16),
            pltpu.VMEM((4, ROPE, D), BF16),
            pltpu.VMEM((HLOC, NOPE, LAT), BF16),
            pltpu.VMEM((HLOC, LAT, VAL), BF16),
            pltpu.VMEM((HLOC, VAL, D), BF16),
            pltpu.VMEM((48, 16, 512), BF16),
            pltpu.VMEM((4, 64, 256), BF16),
            pltpu.VMEM((4, 64, 256), BF16),
            pltpu.VMEM((4, 4, 64, QW), BF16),
            pltpu.VMEM((4, 4, 4, 16, LAT), F32),
            pltpu.VMEM((4, 4, 16, 128), F32),
            pltpu.VMEM((4, 2, 4, 16, LAT), F32),
            pltpu.VMEM((4, 2, 16, 128), F32),
        ]
        for _ in range(2):
            scratch += [pltpu.VMEM((4, 4, 16, LAT), F32), pltpu.VMEM((4, 16, 128), F32)]
        scratch += [
            pltpu.VMEM((2, 4, QUART), F32),
            pltpu.VMEM((2, 4, QUART), F32),
            pltpu.VMEM((2, 2, 4, QUART), F32),
            pltpu.VMEM((4, 4, 4, QUART), BF16),
            pltpu.VMEM((4, D), F32),
            pltpu.VMEM((ROWS, D), F32),
            dma((6,)), dma((NCH,)), dma((4,)),
            dma((3,)), dma((4,)),
            dma((4, 3)), dma((4, 4)),
            dma((4, 4)), dma((4, 4)),
            dma((4, 2)), dma((4, 2)),
            dma((4, 2)), dma((4, 2)),
            dma((2,)), dma((2,)), dma((2,)), dma((2,)),
            dma((2, 7)), dma((2, 7)),
        ]
        return pl.pallas_call(
            kernel,
            out_shape=pltpu.VMEM((ROWS, D), BF16),
            in_specs=[pl.BlockSpec(memory_space=pltpu.SMEM)] + [anyspec] * 8,
            out_specs=pl.BlockSpec(memory_space=pltpu.VMEM),
            scratch_shapes=scratch,
            compiler_params=pltpu.CompilerParams(collective_id=0, has_side_effects=True,
                                                 vmem_limit_bytes=66_000_000),
        )(lengths, hidden, latent_cache, rope_t, w_uq, wqr_t, w_uk, w_uv, w_out)

    row_spec, cache_spec = P('batch', None), P('batch', ('ctx', 'seq'), None)
    head_spec, proj_spec = P('seq', None, None), P(None, 'seq', None)
    return jax.shard_map(local_step, mesh=mesh,
                         in_specs=(row_spec, P('batch'), cache_spec, cache_spec, proj_spec, proj_spec, head_spec, head_spec, head_spec),
                         out_specs=row_spec, check_vma=False)
```

time: 233 us -> 56.9 us (0.24)
  waiting for transfers between devices: 113 us -> 0 us
  Pallas kernels: 0 us -> 56.1 us
  blocking collectives: 53.9 us -> 0 us
  matrix products: 47 us -> 0 us
  between operations: 13.3 us -> 0.01 us
  other arithmetic: 3.59 us -> 0 us
    psum x2 -> x0, waiting for transfers between devices: 60.9 us -> none  [the longest x1 32.5 us: local_step(): mixed = lax.psum(mixed_part, 'seq')]
    pallas_call x0 -> x1, Pallas kernels: none -> 56.1 us  [local_step(): pl.pallas_call(kernel, out_shape=pltpu.VMEM((ROWS, D), BF16), in_specs=[p...]
    dot_general x7 -> x0, matrix products: 47 us -> none  [the longest x1 11.7 us: local_step(): jnp.einsum('bd,dhk->bhk', hidden, w_uq, preferred_element_type=jnp.float32)]
    pmax x1 -> x0, blocking collectives: 33.1 us -> none  [local_step(): global_max = lax.pmax(local_max, ('ctx', 'seq'))]
    reduce_scatter x1 -> x0, waiting for transfers between devices: 27.6 us -> none  [local_step(): lax.psum_scatter(local_acc * rescale[:, :, None], 'seq', scatter_dimensio...]
    unnamed x6 -> x0, waiting for transfers between devices: 22 us -> none
    psum x1 -> x0, blocking collectives: 12 us -> none  [local_step(): sum_heads = lax.psum(sum_heads, 'ctx')]
    all_gather x1 -> x0, blocking collectives: 8.83 us -> none  [local_step(): rope_all = lax.all_gather(q_rope, 'seq', axis=1, tiled=True)]
  transfers between devices with their start and end apart: 5 -> 0, of which waited for: 5 -> 0; matrix products, arithmetic and copies ran while one was open for 5% -> 0% of each run, Pallas kernels for 0% -> 0%
where the time goes in v2:
time: 56.9 us; the launch traced here: 56.8 us
  Pallas kernels  56.1 us (99%)
  local copies, waits for them, and re-layouts  0.68 us (1%)
    pallas_call x1, Pallas kernels, local_step(): pl.pallas_call(kernel, out_shape=pltpu.VMEM((ROWS, D), BF16), in_specs=[p...  56.1 us

profile of v2, /device:TPU:0, one launch (start us, length us, event | category | flops | bytes accessed | tf_op | source)
XLA Modules:
  0.0 56.8 jit_solution(3905049491155771195)
XLA Ops:
  0.0 56.1 %shard_map.91 = bf16[16,6144]{1,0:T(8,128)(2,1)S(1)} custom-call(s32[16]{0:T(128)} %len_ref.1, bf16[16,6144]{1,0:T(8,128)(2,1)} %hid_hbm.1, bf16[16,512,512]{2,1,0:T(8,128)(2,1)} %cache_hbm.1, bf16[16,64,512]{2,1,0:T(8,128)(2,1)} %bitcast.3, bf16[6144,16,128]{2,1,0:T(8,128)(2,1)} %wuq_hbm.1, bf16[16,64,6144]{2,1,0:T(8,128)(2,1)} %bitcast.2, ...), custom_call_target="tpu_custom_call" | custom-call | tf_op jit(solution)/shard_map/pallas_call | solution.py:343
  56.1 0.7 %copy.11 = bf16[16,6144]{1,0:T(8,128)(2,1)} copy(bf16[16,6144]{1,0:T(8,128)(2,1)S(1)} %shard_map.91) | data formatting | bytes 393216

commit v3 on v2

v3 whole, which is shorter than its diff:
```python
import functools

import jax
import jax.numpy as jnp
from jax import lax
from jax.experimental import pallas as pl
from jax.experimental.pallas import tpu as pltpu
from jax.sharding import PartitionSpec as P

MESH = pl.DeviceIdType.MESH
F32, BF16 = jnp.float32, jnp.bfloat16
NEG = -3.0e38

ROWS, D, HLOC, NOPE, ROPE, LAT, VAL = 16, 6144, 16, 128, 64, 512, 128
TLOC = 512
QW = LAT + 128
CH = 1536
NCH = D // CH
BLK = CH // 128
QUART = D // 4


def mm(a, b):
    return lax.dot_general(a, b, (((1,), (0,)), ((), ())), preferred_element_type=F32)


def mm_nt(a, b):
    return lax.dot_general(a, b, (((1,), (1,)), ((), ())), preferred_element_type=F32)


def onehot(shape, fn):
    i = lax.broadcasted_iota(jnp.int32, shape, 0)
    j = lax.broadcasted_iota(jnp.int32, shape, 1)
    return jnp.where(fn(i, j), 1.0, 0.0).astype(BF16)


def pack(ms, ls):
    lane = lax.broadcasted_iota(jnp.int32, (8, 128), 1)
    t = jnp.zeros((8, 128), F32)
    for i in range(2):
        for at, v in ((i, ms[i][0:8]), (2 + i, ms[i][8:16]), (4 + i, ls[i][0:8]), (6 + i, ls[i][8:16])):
            t = jnp.where(lane == at, v, t)
    return t


def unpack(t, i):
    return [jnp.concatenate([t[:, at + i:at + i + 1], t[:, at + 2 + i:at + 3 + i]], axis=0) for at in (0, 4)]


def merge(parts, tiles):
    out, nm, nl = [], [], []
    for i in range(2):
        mls = [unpack(t, i) for t in tiles]
        m = functools.reduce(jnp.maximum, [v[0] for v in mls])
        fs = [jnp.exp(v[0] - m) for v in mls]
        nl.append(functools.reduce(jnp.add, [v[1] * f for v, f in zip(mls, fs)]))
        nm.append(m)
        out.append(functools.reduce(jnp.add, [p(i) * f for p, f in zip(parts, fs)]))
    return out, nm, nl


def kernel(len_ref, hid_hbm, cache_hbm, rope_hbm, wuq_hbm, wqr_hbm, wuk_hbm, wuv_hbm, wout_hbm, out_ref,
           hid, cache, rope, wuq, wqr, wuk, wuv, wout, rep, zq, xq, qg, acc, ml, racc, rml, yra, yrm, zra, zrm,
           yb, yr, tr, fin, hsel, outf,
           lsem, usem, csem, q_s, q_r, a_s, a_r, d_s, d_r, y_s, y_r, z_s, z_r, e_s, e_r, t_s, t_r, f_s, f_r):
    x = lax.axis_index("batch")
    z = lax.axis_index("ctx")
    s = lax.axis_index("seq")
    y, k = s // 2, s % 2
    sp = s + 1 - 2 * k
    sy = s + 2 - 4 * y
    spy = sp + 2 - 4 * y
    zx = {1: z + 1 - 2 * (z % 2), 2: z + 2 - 4 * (z // 2), 3: 3 - z}
    inner = ((z + 1) // 2) % 2
    gs = [3 * (1 - z // 2), 2 - z // 2, zx[1], z]

    dev_p, dev_y = (x, z, sp), (x, z, sy)
    dev_z = {j: (x, zx[j], s) for j in zx}
    peers = [dev_p, dev_y, dev_z[1], dev_z[2], dev_z[3]]

    def local(src, dst, sem):
        c = pltpu.make_async_copy(src, dst, sem)
        c.start()
        return c

    def remote(src, dst, ss, rs, dev):
        return pltpu.make_async_remote_copy(src_ref=src, dst_ref=dst, send_sem=ss, recv_sem=rs,
                                            device_id=dev, device_id_type=MESH)

    started = []

    def go(c):
        c.start()
        started.append(c)

    own4 = pl.ds(pl.multiple_of(4 * z, 4), 4)
    c_hid = local(hid_hbm, hid, lsem.at[0])

    def load_uq(i):
        return local(wuq_hbm.at[pl.ds(i * CH, CH), own4, :], wuq.at[i], usem.at[i])

    c_qr = local(wqr_hbm.at[own4], wqr, lsem.at[1])
    c_uq = [load_uq(i) for i in range(NCH)]
    c_uk = local(wuk_hbm, wuk, lsem.at[2])

    barrier = pltpu.get_barrier_semaphore()
    for d in peers:
        pl.semaphore_signal(barrier, inc=1, device_id=d, device_id_type=MESH)

    spread = onehot((128, 512), lambda i, j: j // 4 == i)
    lane = lax.broadcasted_iota(jnp.int32, (16, 128), 1)
    masks = [jnp.where(lane % 4 == h, 1.0, 0.0).astype(BF16) for h in range(4)]
    wide = [jnp.concatenate([m] * (CH * 4 // 128), axis=1) for m in masks]
    c_hid.wait()
    for t in range(NCH):
        blk = jnp.concatenate([hid[:, (BLK * t + i) * 128:(BLK * t + i + 1) * 128] for i in range(BLK)], axis=0)
        rep[pl.ds(BLK * t, BLK)] = mm(blk, spread).astype(BF16).reshape(BLK, 16, 512)
    c_qr.wait()
    half = D // 2
    qr = (mm_nt(hid[:, :half], wqr[:, :, :half].reshape(4 * ROPE, half))
          + mm_nt(hid[:, half:], wqr[:, :, half:].reshape(4 * ROPE, half))).astype(BF16)
    zq[z, 64:80] = qr[:, :128]
    zq[z, 80:96] = qr[:, 128:]
    qn = jnp.zeros((64, NOPE), F32)
    for i in range(NCH):
        c_uq[i].wait()
        r = jnp.concatenate([rep[i * BLK + t] for t in range(BLK)], axis=1)
        lhs = jnp.concatenate([r * m for m in wide], axis=0)
        qn = qn + mm(lhs, wuq[i].reshape(CH * 4, NOPE))
    zq[z, 0:64] = qn.astype(BF16)
    c_rope = local(rope_hbm, rope, lsem.at[3])
    c_cache = [local(cache_hbm.at[pl.ds(4 * g, 4)], cache.at[pl.ds(4 * g, 4)], csem.at[n]) for n, g in enumerate(gs)]
    c_uv = local(wuv_hbm, wuv, lsem.at[4])
    c_out = local(wout_hbm, wout, lsem.at[5])

    pl.semaphore_wait(barrier, len(peers))
    for j in (3, 2, 1):
        go(remote(zq.at[z], zq.at[z], q_s.at[j - 1], q_r.at[z], dev_z[j]))
    pick = onehot((16, 16), lambda i, j: 4 * z + i == j)
    hsel[...] = mm(pick, hid[...])[0:4]

    def row_of(i):
        return sum((jnp.where(i // 4 == n, 4 * g, 0) for n, g in enumerate(gs))) + i % 4

    perm = onehot((256, 256), lambda i, j: (i % 16) * 16 + row_of(i // 16) == j)

    def latent(zz):
        for h in range(4):
            ql = mm(zq[zz, 16 * h:16 * h + 16], wuk[4 * zz + h]).astype(BF16)
            t = zq[zz, 64 + 16 * (h // 2):80 + 16 * (h // 2)]
            if h % 2:
                t = jnp.concatenate([t[:, 64:], t[:, :64]], axis=1)
            xq[4 * zz + h] = jnp.concatenate([ql, t], axis=1)

    c_uk.wait()
    latent(z)
    for j in (1, 2, 3):
        remote(zq.at[zx[j]], zq.at[zx[j]], q_s.at[0], q_r.at[zx[j]], dev_p).wait_recv()
        latent(zx[j])
    qp = mm(perm, xq[...].reshape(256, QW)).astype(BF16)
    for u in range(8):
        qg[u, s] = qp[32 * u:32 * u + 32]
    for u in range(8):
        go(remote(qg.at[u, s], qg.at[u, s], a_s.at[u, 0], a_r.at[u, s], dev_y))
        go(remote(qg.at[u, s], qg.at[u, s], a_s.at[u, 1], a_r.at[u, s], dev_p))

    def arrived(u, who):
        remote(qg.at[u, who], qg.at[u, who], a_s.at[u, 0], a_r.at[u, who], dev_p).wait_recv()

    def forward(u):
        arrived(u, sy)
        go(remote(qg.at[u, sy], qg.at[u, sy], a_s.at[u, 2], a_r.at[u, sy], dev_p))

    scale = (NOPE + ROPE) ** -0.5
    t0 = (z * 4 + s) * TLOC

    def attend(u):
        bs = [4 * gs[u // 2] + 2 * (u % 2) + i for i in range(2)]
        sc, ws, ms, ls = [], [], [], []
        for i, b in enumerate(bs):
            q = jnp.concatenate([qg[u, p, 16 * i:16 * i + 16, :] for p in range(4)], axis=0)
            sc.append(mm_nt(q[:, :LAT], cache[b]) + mm(q[:, LAT:LAT + ROPE], rope[b]))
        for i, b in enumerate(bs):
            valid = lax.broadcasted_iota(jnp.int32, (64, TLOC), 1) < len_ref[b] - t0
            v = jnp.where(valid, sc[i] * scale, NEG)
            m = jnp.max(v, axis=1, keepdims=True)
            w = jnp.where(valid, jnp.exp(v - m), 0.0)
            ms.append(m)
            ls.append(jnp.sum(w, axis=1, keepdims=True))
            ws.append(w.astype(BF16))
        for i, b in enumerate(bs):
            o = mm(ws[i], cache[b])
            for p in range(4):
                acc[u, p % 2, p // 2, i] = o[16 * p:16 * p + 16]
        for p in range(4):
            cut = slice(16 * p, 16 * p + 16)
            ml[u, p % 2, p // 2] = pack([m[cut] for m in ms], [l[cut] for l in ls])

    def d_copies(u):
        return [remote(acc.at[u, 1 - k], racc.at[u], d_s.at[u, 0], d_r.at[u, 0], dev_p),
                remote(ml.at[u, 1 - k], rml.at[u], d_s.at[u, 1], d_r.at[u, 1], dev_p)]

    def y_copies(u):
        return [remote(acc.at[u, k, 1 - y], yra.at[u], y_s.at[u, 0], y_r.at[u, 0], dev_y),
                remote(ml.at[u, k, 1 - y], yrm.at[u], y_s.at[u, 1], y_r.at[u, 1], dev_y)]

    def z_copies(u):
        n, h = u // 2, u % 2
        to = zx[1] if n == 2 else inner * gs[n] + (1 - inner) * zx[1]
        at = 2 if n == 2 else inner * 3 + (1 - inner) * n
        return [remote(acc.at[u, k, y], zra.at[at, h], z_s.at[u, 0], z_r.at[at, h, 0], (x, to, s)),
                remote(ml.at[u, k, y], zrm.at[at, h], z_s.at[u, 1], z_r.at[at, h, 1], (x, to, s))]

    def z_wait(at, h):
        remote(zra.at[at, h], zra.at[at, h], z_s.at[0, 0], z_r.at[at, h, 0], dev_p).wait_recv()
        remote(zrm.at[at, h], zrm.at[at, h], z_s.at[0, 1], z_r.at[at, h, 1], dev_p).wait_recv()

    def add(u, yy, ra, rm):
        out, m, l = merge([lambda i: acc[u, k, yy, i], ra], [ml[u, k, yy], rm])
        for i in range(2):
            acc[u, k, yy, i] = out[i]
        ml[u, k, yy] = pack(m, l)

    def stage_a(u):
        arrived(u, sp)
        arrived(u, spy)
        if u < 7:
            forward(u + 1)
        if u % 2 == 0:
            c_cache[u // 2].wait()
        attend(u)
        for c in d_copies(u):
            go(c)

    def stage_y(u):
        for c in d_copies(u):
            c.wait_recv()
        add(u, 1 - y, lambda i: racc[u, 1 - y, i], rml[u, 1 - y])
        for c in y_copies(u):
            go(c)
        add(u, y, lambda i: racc[u, y, i], rml[u, y])

    def stage_z(u):
        for c in y_copies(u):
            c.wait_recv()
        add(u, y, lambda i: yra[u, i], yrm[u])
        if u < 4:
            @pl.when(inner == 0)
            def _():
                for c in z_copies(u):
                    c.start()
        elif u < 6:
            for c in z_copies(u):
                go(c)

    def stage_c(u):
        @pl.when(inner == 1)
        def _():
            n, h = u // 2, u % 2
            z_wait(n, h)
            add(u, y, lambda i: zra[n, h, i], zrm[n, h])
            for c in z_copies(u):
                c.start()

    forward(0)
    c_rope.wait()
    plan = []
    for u in range(8):
        ready = 1.2 * (u + 5) if u < 4 else 1.47 * u + 4.9
        plan += [(1.2 * u, stage_a, u), (1.2 * (u + 1) + 0.1, stage_y, u), (ready, stage_z, u)]
        if u < 4:
            plan.append((ready + 3.6, stage_c, u))
    for _, stage, u in sorted(plan, key=lambda e: e[0]):
        stage(u)

    for at in (2, 3):
        for h in range(2):
            z_wait(at, h)
    c_uv.wait()
    c_out.wait()
    ol = []
    for h in range(2):
        u = 6 + h
        out, m, l = merge([lambda i: acc[u, k, y, i], lambda i: zra[2, h, i], lambda i: zra[3, h, i]],
                          [ml[u, k, y], zrm[2, h], zrm[3, h]])
        ol += [(out[i] / l[i]).astype(BF16) for i in range(2)]
    ol = jnp.concatenate(ol, axis=0)
    vs = []
    head = lax.broadcasted_iota(jnp.int32, (64, VAL), 0) % 16
    for h in range(HLOC):
        vs.append(jnp.where(head == h, mm(ol, wuv[h]), 0.0).astype(BF16))
    v = jnp.concatenate(vs, axis=1)
    fold = onehot((16, 64), lambda i, j: j // 16 == i)
    v = mm(fold, v).astype(BF16)

    def cols(c):
        at = pl.multiple_of(c * QUART, QUART)
        return mm(v, wout[:, :, pl.ds(at, QUART)].reshape(HLOC * VAL, QUART))[0:4]

    def e_copy(n):
        return remote(yb.at[n], yr.at[n], e_s.at[n], e_r.at[n], dev_p)

    def t_copy(n):
        return remote(tr.at[0, n], tr.at[1, n], t_s.at[n], t_r.at[n], dev_y)

    def finish(n):
        t_copy(n).wait_recv()
        c = 2 * k + n
        res = hsel[:, pl.ds(pl.multiple_of(c * QUART, QUART), QUART)] + (tr[0, n] + tr[1, n])
        fin[z, c] = res.astype(BF16)
        for j in (3, 2, 1):
            go(remote(fin.at[z, c], fin.at[z, c], f_s.at[n, j], f_r.at[n, j], dev_z[j]))
        go(remote(fin.at[z, c], fin.at[z, c], f_s.at[n, 0], f_r.at[n, 0], dev_p))

    for n in range(2):
        yb[n] = cols(2 * (1 - k) + n)
        go(e_copy(n))
    for n in range(2):
        part = cols(2 * k + n)
        e_copy(n).wait_recv()
        tr[0, n] = part + yr[n]
        go(t_copy(n))
        if n:
            finish(0)
    finish(1)
    for n in range(2):
        for j in (1, 2, 3):
            at = fin.at[zx[j], 2 * k + n]
            remote(at, at, f_s.at[n, 0], f_r.at[n, j], dev_p).wait_recv()
            go(remote(at, at, f_s.at[n, 3 + j], f_r.at[n, 3 + j], dev_p))
    for n in range(2):
        for j, zz in enumerate((z, zx[1], zx[2], zx[3])):
            at = fin.at[zz, 2 * (1 - k) + n]
            remote(at, at, f_s.at[n, 0], f_r.at[n, 3 + j if j else 0], dev_p).wait_recv()
    for i in range(4):
        for c in range(4):
            outf[4 * i:4 * i + 4, c * QUART:(c + 1) * QUART] = fin[i, c].astype(F32)
    out_ref[...] = outf[...].astype(BF16)
    for c in started:
        c.wait_send()
    for u in range(4):
        for c in z_copies(u):
            c.wait_send()


def solution(mesh):
    def local_step(hidden, lengths, latent_cache, rope_keys, w_uq, w_qr, w_uk, w_uv, w_out):
        rope_t = jnp.transpose(rope_keys, (0, 2, 1))
        wqr_t = jnp.transpose(w_qr, (1, 2, 0))
        anyspec = pl.BlockSpec(memory_space=pl.ANY)
        dma = pltpu.SemaphoreType.DMA
        scratch = [
            pltpu.VMEM((ROWS, D), BF16),
            pltpu.VMEM((ROWS, TLOC, LAT), BF16),
            pltpu.VMEM((ROWS, ROPE, TLOC), BF16),
            pltpu.VMEM((NCH, CH, 4, NOPE), BF16),
            pltpu.VMEM((4, ROPE, D), BF16),
            pltpu.VMEM((HLOC, NOPE, LAT), BF16),
            pltpu.VMEM((HLOC, LAT, VAL), BF16),
            pltpu.VMEM((HLOC, VAL, D), BF16),
            pltpu.VMEM((48, 16, 512), BF16),
            pltpu.VMEM((4, 96, 128), BF16),
            pltpu.VMEM((HLOC, 16, QW), BF16),
            pltpu.VMEM((8, 4, 32, QW), BF16),
            pltpu.VMEM((8, 2, 2, 2, 16, LAT), F32),
            pltpu.VMEM((8, 2, 2, 8, 128), F32),
            pltpu.VMEM((8, 2, 2, 16, LAT), F32),
            pltpu.VMEM((8, 2, 8, 128), F32),
            pltpu.VMEM((8, 2, 16, LAT), F32),
            pltpu.VMEM((8, 8, 128), F32),
            pltpu.VMEM((4, 2, 2, 16, LAT), F32),
            pltpu.VMEM((4, 2, 8, 128), F32),
            pltpu.VMEM((2, 4, QUART), F32),
            pltpu.VMEM((2, 4, QUART), F32),
            pltpu.VMEM((2, 2, 4, QUART), F32),
            pltpu.VMEM((4, 4, 4, QUART), BF16),
            pltpu.VMEM((4, D), F32),
            pltpu.VMEM((ROWS, D), F32),
            dma((6,)), dma((NCH,)), dma((4,)),
            dma((3,)), dma((4,)),
            dma((8, 3)), dma((8, 4)),
            dma((8, 2)), dma((8, 2)),
            dma((8, 2)), dma((8, 2)),
            dma((8, 2)), dma((4, 2, 2)),
            dma((2,)), dma((2,)), dma((2,)), dma((2,)),
            dma((2, 7)), dma((2, 7)),
        ]
        return pl.pallas_call(
            kernel,
            out_shape=pltpu.VMEM((ROWS, D), BF16),
            in_specs=[pl.BlockSpec(memory_space=pltpu.SMEM)] + [anyspec] * 8,
            out_specs=pl.BlockSpec(memory_space=pltpu.VMEM),
            scratch_shapes=scratch,
            compiler_params=pltpu.CompilerParams(collective_id=0, has_side_effects=True,
                                                 vmem_limit_bytes=66_000_000),
        )(lengths, hidden, latent_cache, rope_t, w_uq, wqr_t, w_uk, w_uv, w_out)

    row_spec, cache_spec = P('batch', None), P('batch', ('ctx', 'seq'), None)
    head_spec, proj_spec = P('seq', None, None), P(None, 'seq', None)
    return jax.shard_map(local_step, mesh=mesh,
                         in_specs=(row_spec, P('batch'), cache_spec, cache_spec, proj_spec, proj_spec, head_spec, head_spec, head_spec),
                         out_specs=row_spec, check_vma=False)
```

time: 56.9 us -> 53.4 us (0.938)
  Pallas kernels: 56.1 us -> 52.6 us
    pallas_call x1, Pallas kernels: 56.1 us -> 52.6 us  [local_step(): pl.pallas_call(kernel, out_shape=pltpu.VMEM((ROWS, D), BF16), in_specs=[p...]
where the time goes in v3:
time: 53.4 us; the launch traced here: 53.3 us
  Pallas kernels  52.6 us (99%)
  local copies, waits for them, and re-layouts  0.68 us (1%)
    pallas_call x1, Pallas kernels, local_step(): pl.pallas_call(kernel, out_shape=pltpu.VMEM((ROWS, D), BF16), in_specs=[p...  52.6 us

profile of v3, /device:TPU:0, one launch (start us, length us, event | category | flops | bytes accessed | tf_op | source)
XLA Modules:
  0.0 53.3 jit_solution(16081504136298798238)
XLA Ops:
  0.0 52.6 %shard_map.91 = bf16[16,6144]{1,0:T(8,128)(2,1)S(1)} custom-call(s32[16]{0:T(128)} %len_ref.1, bf16[16,6144]{1,0:T(8,128)(2,1)} %hid_hbm.1, bf16[16,512,512]{2,1,0:T(8,128)(2,1)} %cache_hbm.1, bf16[16,64,512]{2,1,0:T(8,128)(2,1)} %bitcast.3, bf16[6144,16,128]{2,1,0:T(8,128)(2,1)} %wuq_hbm.1, bf16[16,64,6144]{2,1,0:T(8,128)(2,1)} %bitcast.2, ...), custom_call_target="tpu_custom_call" | custom-call | tf_op jit(solution)/shard_map/pallas_call | solution.py:388
  52.6 0.7 %copy.11 = bf16[16,6144]{1,0:T(8,128)(2,1)} copy(bf16[16,6144]{1,0:T(8,128)(2,1)S(1)} %shard_map.91) | data formatting | bytes 393216

commit v4 on v3

v4 whole, which is shorter than its diff:
```python
import functools

import jax
import jax.numpy as jnp
from jax import lax
from jax.experimental import pallas as pl
from jax.experimental.pallas import tpu as pltpu
from jax.sharding import PartitionSpec as P

MESH = pl.DeviceIdType.MESH
F32, BF16 = jnp.float32, jnp.bfloat16
NEG = -3.0e38

ROWS, D, HLOC, NOPE, ROPE, LAT, VAL = 16, 6144, 16, 128, 64, 512, 128
TLOC = 512
QW = LAT + 128
CH = 1536
NCH = D // CH
BLK = CH // 128
QUART = D // 4
PACE = 1.2


def mm(a, b):
    return lax.dot_general(a, b, (((1,), (0,)), ((), ())), preferred_element_type=F32)


def mm_nt(a, b):
    return lax.dot_general(a, b, (((1,), (1,)), ((), ())), preferred_element_type=F32)


def onehot(shape, fn):
    i = lax.broadcasted_iota(jnp.int32, shape, 0)
    j = lax.broadcasted_iota(jnp.int32, shape, 1)
    return jnp.where(fn(i, j), 1.0, 0.0).astype(BF16)


def pack(ms, ls):
    lane = lax.broadcasted_iota(jnp.int32, (8, 128), 1)
    t = jnp.zeros((8, 128), F32)
    for i in range(2):
        for at, v in ((i, ms[i][0:8]), (2 + i, ms[i][8:16]), (4 + i, ls[i][0:8]), (6 + i, ls[i][8:16])):
            t = jnp.where(lane == at, v, t)
    return t


def unpack(t, i):
    return [jnp.concatenate([t[:, at + i:at + i + 1], t[:, at + 2 + i:at + 3 + i]], axis=0) for at in (0, 4)]


def merge(refs):
    out, nm, nl = [], [], []
    tiles = [r[128:136] for r in refs]
    for i in range(2):
        mls = [unpack(t, i) for t in tiles]
        m = functools.reduce(jnp.maximum, [v[0] for v in mls])
        fs = [jnp.exp(v[0] - m) for v in mls]
        nl.append(functools.reduce(jnp.add, [v[1] * f for v, f in zip(mls, fs)]))
        nm.append(m)
        for c in range(4):
            at = 16 * (4 * i + c)
            out.append(functools.reduce(jnp.add, [r[at:at + 16] * f for r, f in zip(refs, fs)]))
    return out, nm, nl


def kernel(len_ref, hid_hbm, cache_hbm, rope_hbm, wuq_hbm, wqr_hbm, wuk_hbm, wuv_hbm, wout_hbm, out_ref,
           hid, cache, rope, wuq, wqr, wuk, wuv, wout, rep, zq, xq, qg, sbuf, acc, racc, yra, zra,
           yb, yr, tr, fin, hsel, outf,
           lsem, usem, csem, q_s, q_r, a_s, a_r, d_s, d_r, y_s, y_r, z_s, z_r, e_s, e_r, t_s, t_r, f_s, f_r):
    x = lax.axis_index("batch")
    z = lax.axis_index("ctx")
    s = lax.axis_index("seq")
    y, k = s // 2, s % 2
    sp = s + 1 - 2 * k
    sy = s + 2 - 4 * y
    spy = sp + 2 - 4 * y
    zx = {1: z + 1 - 2 * (z % 2), 2: z + 2 - 4 * (z // 2), 3: 3 - z}
    inner = ((z + 1) // 2) % 2
    gs = [3 * (1 - z // 2), 2 - z // 2, zx[1], z]

    dev_p, dev_y = (x, z, sp), (x, z, sy)
    dev_z = {j: (x, zx[j], s) for j in zx}
    peers = [dev_p, dev_y, dev_z[1], dev_z[2], dev_z[3]]

    def local(src, dst, sem, priority=1):
        c = pltpu.make_async_copy(src, dst, sem)
        c.start(priority=priority)
        return c

    def remote(src, dst, ss, rs, dev):
        return pltpu.make_async_remote_copy(src_ref=src, dst_ref=dst, send_sem=ss, recv_sem=rs,
                                            device_id=dev, device_id_type=MESH)

    def go(c):
        c.start()

    own4 = pl.ds(pl.multiple_of(4 * z, 4), 4)
    c_hid = local(hid_hbm, hid, lsem.at[0], 0)

    def load_uq(i):
        return local(wuq_hbm.at[pl.ds(i * CH, CH), own4, :], wuq.at[i], usem.at[i])

    c_uq = [load_uq(i) for i in range(NCH)]
    c_qr = local(wqr_hbm.at[own4], wqr, lsem.at[1])

    barrier = pltpu.get_barrier_semaphore()
    for d in peers:
        pl.semaphore_signal(barrier, inc=1, device_id=d, device_id_type=MESH)

    spread = onehot((128, 512), lambda i, j: j // 4 == i)
    lane = lax.broadcasted_iota(jnp.int32, (16, 128), 1)
    masks = [jnp.where(lane % 4 == h, 1.0, 0.0).astype(BF16) for h in range(4)]
    wide = [jnp.concatenate([m] * (CH * 4 // 128), axis=1) for m in masks]
    c_hid.wait()
    for t in range(NCH):
        blk = jnp.concatenate([hid[:, (BLK * t + i) * 128:(BLK * t + i + 1) * 128] for i in range(BLK)], axis=0)
        rep[pl.ds(BLK * t, BLK)] = mm(blk, spread).astype(BF16).reshape(BLK, 16, 512)
    qn = [jnp.zeros((64, NOPE), F32)] * 2
    for i in range(0, NCH, 2):
        c_uq[i].wait()
        c_uq[i + 1].wait()
        for part in range(2):
            for n in range(2):
                at, size = part * (BLK // 2), BLK // 2
                r = jnp.concatenate([rep[(i + n) * BLK + at + t] for t in range(size)], axis=1)
                lhs = jnp.concatenate([r * m[:, :size * 512] for m in wide], axis=0)
                qn[n] = qn[n] + mm(lhs, wuq[i + n, at * 128:(at + size) * 128].reshape(size * 512, NOPE))
        if i == 0:
            c_uk = local(wuk_hbm, wuk, lsem.at[2])
    c_qr.wait()
    qr = jnp.concatenate([mm_nt(hid[...], wqr[2 * h:2 * h + 2].reshape(2 * ROPE, D)) for h in range(2)], axis=1)
    qr = qr.astype(BF16)
    zq[z, 64:80] = qr[:, :128]
    zq[z, 80:96] = qr[:, 128:]
    zq[z, 0:64] = (qn[0] + qn[1]).astype(BF16)
    c_rope = local(rope_hbm, rope, lsem.at[3])
    c_cache = local(cache_hbm, cache, csem.at[0])
    c_uv = local(wuv_hbm, wuv, lsem.at[4])
    c_out = local(wout_hbm, wout, lsem.at[5])

    pl.semaphore_wait(barrier, len(peers))
    def give_z():
        for j in (3, 2, 1):
            remote(zq.at[z], zq.at[z], q_s.at[0], q_r.at[z], dev_z[j]).start()

    give_z()
    pick = onehot((16, 16), lambda i, j: 4 * z + i == j)
    hsel[...] = mm(pick, hid[...])[0:4]

    def row_of(i):
        return sum((jnp.where(i // 4 == n, 4 * g, 0) for n, g in enumerate(gs))) + i % 4

    perm = onehot((256, 256), lambda i, j: (i % 16) * 16 + row_of(i // 16) == j)

    def latent(zz):
        for h in range(4):
            ql = mm(zq[zz, 16 * h:16 * h + 16], wuk[4 * zz + h]).astype(BF16)
            t = zq[zz, 64 + 16 * (h // 2):80 + 16 * (h // 2)]
            if h % 2:
                t = jnp.concatenate([t[:, 64:], t[:, :64]], axis=1)
            xq[4 * zz + h] = jnp.concatenate([ql, t], axis=1)

    c_uk.wait()
    latent(z)
    for j in (1, 2, 3):
        remote(zq.at[zx[j]], zq.at[zx[j]], q_s.at[0], q_r.at[zx[j]], dev_p).wait_recv()
        latent(zx[j])
    qp = mm(perm, xq[...].reshape(256, QW)).astype(BF16)
    for u in range(8):
        qg[u, 0] = qp[32 * u:32 * u + 32]
        go(remote(qg.at[u, 0], qg.at[u, 1], a_s.at[0], a_r.at[u, 0], dev_y))
        go(remote(qg.at[u, 0], qg.at[u, 2], a_s.at[1], a_r.at[u, 1], dev_p))

    def arrived(u, n):
        remote(qg.at[u, n], qg.at[u, n], a_s.at[0], a_r.at[u, n - 1], dev_p).wait_recv()

    def forward(u):
        arrived(u, 1)
        go(remote(qg.at[u, 1], qg.at[u, 3], a_s.at[2], a_r.at[u, 2], dev_p))

    scale = (NOPE + ROPE) ** -0.5
    t0 = (z * 4 + s) * TLOC

    def rows_of(u):
        return [4 * gs[u // 2] + 2 * (u % 2) + i for i in range(2)]

    def scores(u):
        for i, b in enumerate(rows_of(u)):
            q = jnp.concatenate([qg[u, p, 16 * i:16 * i + 16, :] for p in range(4)], axis=0)
            sbuf[u % 2, i] = mm_nt(q[:, :LAT], cache[b]) + mm(q[:, LAT:LAT + ROPE], rope[b])

    def attend(u):
        ws, ms, ls = [], [], []
        for i, b in enumerate(rows_of(u)):
            valid = lax.broadcasted_iota(jnp.int32, (64, TLOC), 1) < len_ref[b] - t0
            v = jnp.where(valid, sbuf[u % 2, i] * scale, NEG)
            m = jnp.max(v, axis=1, keepdims=True)
            w = jnp.where(valid, jnp.exp(v - m), 0.0)
            ms.append(m)
            ls.append(jnp.sum(w, axis=1, keepdims=True))
            ws.append(w.astype(BF16))
        for i, b in enumerate(rows_of(u)):
            o = mm(ws[i], cache[b])
            for p in range(4):
                for c in range(4):
                    acc[u, p, 16 * (4 * i + c):16 * (4 * i + c) + 16] = o[16 * p:16 * p + 16, 128 * c:128 * c + 128]
        for p in range(4):
            cut = slice(16 * p, 16 * p + 16)
            acc[u, p, 128:136] = pack([m[cut] for m in ms], [l[cut] for l in ls])

    def d_copy(u):
        return remote(acc.at[u, pl.ds(2, 2)], racc.at[u], d_s.at[0], d_r.at[u], dev_p)

    def y_copy(u):
        return remote(acc.at[u, 1], yra.at[u], y_s.at[0], y_r.at[u], dev_y)

    def z_copy(u):
        n, h = u // 2, u % 2
        to = zx[1] if n == 2 else inner * gs[n] + (1 - inner) * zx[1]
        at = 2 if n == 2 else inner * 3 + (1 - inner) * n
        return remote(acc.at[u, 0], zra.at[at, h], z_s.at[0], z_r.at[at, h], (x, to, s))

    def z_wait(at, h):
        remote(zra.at[at, h], zra.at[at, h], z_s.at[0], z_r.at[at, h], dev_p).wait_recv()

    def add(u, n, other):
        out, m, l = merge([acc[u, n], other])
        for c, o in enumerate(out):
            acc[u, n, 16 * c:16 * c + 16] = o
        acc[u, n, 128:136] = pack(m, l)

    def ready(u):
        arrived(u, 2)
        arrived(u, 3)
        if u < 7:
            forward(u + 1)
        scores(u)

    def stage_r(u):
        ready(u)

    def stage_a(u):
        if 0 < u < 7:
            ready(u + 1)
        attend(u)
        go(d_copy(u))

    def stage_y(u):
        d_copy(u).wait_recv()
        add(u, 1, racc[u, 1])
        go(y_copy(u))
        add(u, 0, racc[u, 0])

    def stage_z(u):
        y_copy(u).wait_recv()
        add(u, 0, yra[u])
        if u < 4:
            @pl.when(inner == 0)
            def _():
                z_copy(u).start()
        elif u < 6:
            go(z_copy(u))

    def stage_c(u):
        @pl.when(inner == 1)
        def _():
            z_wait(u // 2, u % 2)
            add(u, 0, zra[u // 2, u % 2])
            z_copy(u).start()

    forward(0)
    c_rope.wait()
    c_cache.wait()
    plan = [(-1, stage_r, 0), (0.2, stage_r, 1)]
    for u in range(8):
        at = PACE * (u + 5) if u < 4 else 1.47 * u + 4.9
        plan += [(PACE * u, stage_a, u), (PACE * (u + 1) + (0.1 if u else -0.9), stage_y, u), (at, stage_z, u)]
        if u < 4:
            plan.append((at + 3.6, stage_c, u))
    for _, stage, u in sorted(plan, key=lambda e: e[0]):
        stage(u)

    for at in (2, 3):
        for h in range(2):
            z_wait(at, h)
    c_uv.wait()
    c_out.wait()
    ol = []
    for h in range(2):
        u = 6 + h
        out, m, l = merge([acc[u, 0], zra[2, h], zra[3, h]])
        ol += [jnp.concatenate([(out[4 * i + c] / l[i]).astype(BF16) for c in range(4)], axis=1) for i in range(2)]
    ol = jnp.concatenate(ol, axis=0)
    vs = []
    head = lax.broadcasted_iota(jnp.int32, (64, VAL), 0) % 16
    for h in range(HLOC):
        vs.append(jnp.where(head == h, mm(ol, wuv[h]), 0.0).astype(BF16))
    v = jnp.concatenate(vs, axis=1)
    fold = onehot((16, 64), lambda i, j: j // 16 == i)
    v = mm(fold, v).astype(BF16)

    def cols(c):
        return mm(v, wout[:, :, c * QUART:(c + 1) * QUART].reshape(HLOC * VAL, QUART))[0:4]

    def e_copy(c):
        return remote(yb.at[c], yr.at[c % 2], e_s.at[0], e_r.at[c % 2], dev_p)

    def t_copy(n):
        return remote(tr.at[0, n], tr.at[1, n], t_s.at[0], t_r.at[n], dev_y)

    def pair(c):
        n = c % 2
        e_copy(c).wait_recv()
        tr[0, n] = yb[c] + yr[n]
        t_copy(n).start()

    def finish(n):
        t_copy(n).wait_recv()
        c = 2 * k + n
        res = hsel[:, pl.ds(pl.multiple_of(c * QUART, QUART), QUART)] + (tr[0, n] + tr[1, n])
        fin[4 * z + c] = res.astype(BF16)
        for j in (3, 2, 1):
            go(remote(fin.at[4 * z + c], fin.at[4 * z + c], f_s.at[0], f_r.at[n, j], dev_z[j]))
        go(remote(fin.at[4 * z + c], fin.at[4 * z + c], f_s.at[0], f_r.at[n, 0], dev_p))

    for c in range(4):
        yb[c] = cols(c)
        pl.when(k == 1 - c // 2)(lambda: e_copy(c).start())
        if c == 1:
            pl.when(k == 0)(lambda: pair(0))
        elif c == 2:
            pl.when(k == 0)(lambda: pair(1))
        elif c == 3:
            pl.when(k == 1)(lambda: pair(2))
    pl.when(k == 1)(lambda: pair(3))
    for n in range(2):
        finish(n)
    for n in range(2):
        for j in (1, 2, 3):
            at = fin.at[4 * zx[j] + 2 * k + n]
            remote(at, at, f_s.at[0], f_r.at[n, j], dev_p).wait_recv()
            go(remote(at, at, f_s.at[0], f_r.at[n, 3 + j], dev_p))
    for n in range(2):
        for j, zz in enumerate((z, zx[1], zx[2], zx[3])):
            at = fin.at[4 * zz + 2 * (1 - k) + n]
            remote(at, at, f_s.at[0], f_r.at[n, 3 + j if j else 0], dev_p).wait_recv()
    for i in range(4):
        for c in range(4):
            outf[4 * i:4 * i + 4, c * QUART:(c + 1) * QUART] = fin[4 * i + c].astype(F32)
    out_ref[...] = outf[...].astype(BF16)
    for src, sem in ((zq.at[pl.ds(0, 3)], q_s.at[0]), (qg.at[:, 0], a_s.at[0]), (qg.at[:, 0], a_s.at[1]), (qg.at[:, 1], a_s.at[2]),
                     (acc.at[:, pl.ds(2, 2)], d_s.at[0]), (acc.at[:, 1], y_s.at[0]), (acc.at[pl.ds(0, 6), 0], z_s.at[0]),
                     (yb.at[pl.ds(0, 2)], e_s.at[0]), (tr.at[0], t_s.at[0]), (fin.at[pl.ds(0, 14)], f_s.at[0])):
        remote(src, src, sem, d_r.at[0], dev_p).wait_send()


def solution(mesh):
    def local_step(hidden, lengths, latent_cache, rope_keys, w_uq, w_qr, w_uk, w_uv, w_out):
        rope_t = jnp.transpose(rope_keys, (0, 2, 1))
        wqr_t = jnp.transpose(w_qr, (1, 2, 0))
        anyspec = pl.BlockSpec(memory_space=pl.ANY)
        dma = pltpu.SemaphoreType.DMA
        scratch = [
            pltpu.VMEM((ROWS, D), BF16),
            pltpu.VMEM((ROWS, TLOC, LAT), BF16),
            pltpu.VMEM((ROWS, ROPE, TLOC), BF16),
            pltpu.VMEM((NCH, CH, 4, NOPE), BF16),
            pltpu.VMEM((4, ROPE, D), BF16),
            pltpu.VMEM((HLOC, NOPE, LAT), BF16),
            pltpu.VMEM((HLOC, LAT, VAL), BF16),
            pltpu.VMEM((HLOC, VAL, D), BF16),
            pltpu.VMEM((48, 16, 512), BF16),
            pltpu.VMEM((4, 96, 128), BF16),
            pltpu.VMEM((HLOC, 16, QW), BF16),
            pltpu.VMEM((8, 4, 32, QW), BF16),
            pltpu.VMEM((2, 2, 64, TLOC), F32),
            pltpu.VMEM((8, 4, 136, 128), F32),
            pltpu.VMEM((8, 2, 136, 128), F32),
            pltpu.VMEM((8, 136, 128), F32),
            pltpu.VMEM((4, 2, 136, 128), F32),
            pltpu.VMEM((4, 4, QUART), F32),
            pltpu.VMEM((2, 4, QUART), F32),
            pltpu.VMEM((2, 2, 4, QUART), F32),
            pltpu.VMEM((16, 4, QUART), BF16),
            pltpu.VMEM((4, D), F32),
            pltpu.VMEM((ROWS, D), F32),
            dma((6,)), dma((NCH,)), dma((1,)),
            dma((1,)), dma((4,)),
            dma((3,)), dma((8, 3)),
            dma((1,)), dma((8,)),
            dma((1,)), dma((8,)),
            dma((1,)), dma((4, 2)),
            dma((1,)), dma((2,)), dma((1,)), dma((2,)),
            dma((1,)), dma((2, 7)),
        ]
        return pl.pallas_call(
            kernel,
            out_shape=pltpu.VMEM((ROWS, D), BF16),
            in_specs=[pl.BlockSpec(memory_space=pltpu.SMEM)] + [anyspec] * 8,
            out_specs=pl.BlockSpec(memory_space=pltpu.VMEM),
            scratch_shapes=scratch,
            compiler_params=pltpu.CompilerParams(collective_id=0, has_side_effects=True,
                                                 vmem_limit_bytes=66_000_000),
        )(lengths, hidden, latent_cache, rope_t, w_uq, wqr_t, w_uk, w_uv, w_out)

    row_spec, cache_spec = P('batch', None), P('batch', ('ctx', 'seq'), None)
    head_spec, proj_spec = P('seq', None, None), P(None, 'seq', None)
    return jax.shard_map(local_step, mesh=mesh,
                         in_specs=(row_spec, P('batch'), cache_spec, cache_spec, proj_spec, proj_spec, head_spec, head_spec, head_spec),
                         out_specs=row_spec, check_vma=False)
```

time: 53.4 us -> 50.2 us (0.940)
  Pallas kernels: 52.6 us -> 49.4 us
    pallas_call x1, Pallas kernels: 52.6 us -> 49.4 us  [local_step(): pl.pallas_call(kernel, out_shape=pltpu.VMEM((ROWS, D), BF16), in_specs=[p...]
where the time goes in v4:
time: 50.2 us; the launch traced here: 50.1 us
  Pallas kernels  49.4 us (98%)
  local copies, waits for them, and re-layouts  0.68 us (1%)
    pallas_call x1, Pallas kernels, local_step(): pl.pallas_call(kernel, out_shape=pltpu.VMEM((ROWS, D), BF16), in_specs=[p...  49.4 us

profile of v4, /device:TPU:0, one launch (start us, length us, event | category | flops | bytes accessed | tf_op | source)
XLA Modules:
  0.0 50.1 jit_solution(7783590282112114472)
XLA Ops:
  0.0 49.4 %shard_map.91 = bf16[16,6144]{1,0:T(8,128)(2,1)S(1)} custom-call(s32[16]{0:T(128)} %len_ref.1, bf16[16,6144]{1,0:T(8,128)(2,1)} %hid_hbm.1, bf16[16,512,512]{2,1,0:T(8,128)(2,1)} %cache_hbm.1, bf16[16,64,512]{2,1,0:T(8,128)(2,1)} %bitcast.3, bf16[6144,16,128]{2,1,0:T(8,128)(2,1)} %wuq_hbm.1, bf16[16,64,6144]{2,1,0:T(8,128)(2,1)} %bitcast.2, ...), custom_call_target="tpu_custom_call" | custom-call | tf_op jit(solution)/shard_map/pallas_call | solution.py:396
  49.4 0.7 %copy.11 = bf16[16,6144]{1,0:T(8,128)(2,1)} copy(bf16[16,6144]{1,0:T(8,128)(2,1)S(1)} %shard_map.91) | data formatting | bytes 393216

commit v5 on v4

--- a/solution.py
+++ b/solution.py
@@ -19,6 +19,7 @@
 BLK = CH // 128
 QUART = D // 4
 PACE = 1.2
+AHEAD = 5
 
 
 def mm(a, b):
@@ -166,16 +167,22 @@
         remote(zq.at[zx[j]], zq.at[zx[j]], q_s.at[0], q_r.at[zx[j]], dev_p).wait_recv()
         latent(zx[j])
     qp = mm(perm, xq[...].reshape(256, QW)).astype(BF16)
+    def give(u):
+        go(remote(qg.at[u, 0], qg.at[u, 1], a_s.at[0], a_r.at[u, 0], dev_y))
+        go(remote(qg.at[u, 0], qg.at[u, 2], a_s.at[1], a_r.at[u, 1], dev_p))
+
     for u in range(8):
         qg[u, 0] = qp[32 * u:32 * u + 32]
-        go(remote(qg.at[u, 0], qg.at[u, 1], a_s.at[0], a_r.at[u, 0], dev_y))
-        go(remote(qg.at[u, 0], qg.at[u, 2], a_s.at[1], a_r.at[u, 1], dev_p))
+        if u < AHEAD:
+            give(u)
 
     def arrived(u, n):
         remote(qg.at[u, n], qg.at[u, n], a_s.at[0], a_r.at[u, n - 1], dev_p).wait_recv()
 
     def forward(u):
         arrived(u, 1)
+        if u + AHEAD < 8:
+            give(u + AHEAD)
         go(remote(qg.at[u, 1], qg.at[u, 3], a_s.at[2], a_r.at[u, 2], dev_p))
 
     scale = (NOPE + ROPE) ** -0.5
@@ -240,7 +247,7 @@
         ready(u)
 
     def stage_a(u):
-        if 0 < u < 7:
+        if 1 < u < 7:
             ready(u + 1)
         attend(u)
         go(d_copy(u))
@@ -271,13 +278,14 @@
     forward(0)
     c_rope.wait()
     c_cache.wait()
-    plan = [(-1, stage_r, 0), (0.2, stage_r, 1)]
+    plan = [(-1, stage_r, 0), (0.1, stage_r, 1), (0.4, stage_r, 2)]
+    first = {(stage_a, 1): 0.2, (stage_y, 0): 0.3, (stage_y, 1): 0.5}
     for u in range(8):
         at = PACE * (u + 5) if u < 4 else 1.47 * u + 4.9
         plan += [(PACE * u, stage_a, u), (PACE * (u + 1) + (0.1 if u else -0.9), stage_y, u), (at, stage_z, u)]
         if u < 4:
             plan.append((at + 3.6, stage_c, u))
-    for _, stage, u in sorted(plan, key=lambda e: e[0]):
+    for _, stage, u in sorted(plan, key=lambda e: first.get(e[1:], e[0])):
         stage(u)
 
     for at in (2, 3):

time: 50.2 us -> 49.7 us (0.990)
  no operation moved by 1% of the time
where the time goes in v5:
time: 49.7 us; the launch traced here: 49.6 us
  Pallas kernels  48.9 us (98%)
  local copies, waits for them, and re-layouts  0.68 us (1%)
    pallas_call x1, Pallas kernels, local_step(): pl.pallas_call(kernel, out_shape=pltpu.VMEM((ROWS, D), BF16), in_specs=[p...  48.9 us

profile of v5, /device:TPU:0, one launch (start us, length us, event | category | flops | bytes accessed | tf_op | source)
XLA Modules:
  0.0 49.6 jit_solution(11059821129315477560)
XLA Ops:
  0.0 48.9 %shard_map.91 = bf16[16,6144]{1,0:T(8,128)(2,1)S(1)} custom-call(s32[16]{0:T(128)} %len_ref.1, bf16[16,6144]{1,0:T(8,128)(2,1)} %hid_hbm.1, bf16[16,512,512]{2,1,0:T(8,128)(2,1)} %cache_hbm.1, bf16[16,64,512]{2,1,0:T(8,128)(2,1)} %bitcast.3, bf16[6144,16,128]{2,1,0:T(8,128)(2,1)} %wuq_hbm.1, bf16[16,64,6144]{2,1,0:T(8,128)(2,1)} %bitcast.2, ...), custom_call_target="tpu_custom_call" | custom-call | tf_op jit(solution)/shard_map/pallas_call | solution.py:404
  48.9 0.7 %copy.11 = bf16[16,6144]{1,0:T(8,128)(2,1)} copy(bf16[16,6144]{1,0:T(8,128)(2,1)S(1)} %shard_map.91) | data formatting | bytes 393216

commit v6 on v5

--- a/solution.py
+++ b/solution.py
@@ -19,6 +19,7 @@
 BLK = CH // 128
 QUART = D // 4
 PACE = 1.2
+LAG = 3.6
 AHEAD = 5
 
 
@@ -99,9 +100,9 @@
     c_hid = local(hid_hbm, hid, lsem.at[0], 0)
 
     def load_uq(i):
-        return local(wuq_hbm.at[pl.ds(i * CH, CH), own4, :], wuq.at[i], usem.at[i])
-
-    c_uq = [load_uq(i) for i in range(NCH)]
+        return local(wuq_hbm.at[pl.ds(i * 2 * CH, 2 * CH), own4, :], wuq.at[i], usem.at[i])
+
+    c_uq = [load_uq(i) for i in range(NCH // 2)]
     c_qr = local(wqr_hbm.at[own4], wqr, lsem.at[1])
 
     barrier = pltpu.get_barrier_semaphore()
@@ -118,14 +119,13 @@
         rep[pl.ds(BLK * t, BLK)] = mm(blk, spread).astype(BF16).reshape(BLK, 16, 512)
     qn = [jnp.zeros((64, NOPE), F32)] * 2
     for i in range(0, NCH, 2):
-        c_uq[i].wait()
-        c_uq[i + 1].wait()
+        c_uq[i // 2].wait()
         for part in range(2):
             for n in range(2):
                 at, size = part * (BLK // 2), BLK // 2
                 r = jnp.concatenate([rep[(i + n) * BLK + at + t] for t in range(size)], axis=1)
                 lhs = jnp.concatenate([r * m[:, :size * 512] for m in wide], axis=0)
-                qn[n] = qn[n] + mm(lhs, wuq[i + n, at * 128:(at + size) * 128].reshape(size * 512, NOPE))
+                qn[n] = qn[n] + mm(lhs, wuq[i // 2, (n * BLK + at) * 128:(n * BLK + at + size) * 128].reshape(size * 512, NOPE))
         if i == 0:
             c_uk = local(wuk_hbm, wuk, lsem.at[2])
     c_qr.wait()
@@ -135,14 +135,14 @@
     zq[z, 80:96] = qr[:, 128:]
     zq[z, 0:64] = (qn[0] + qn[1]).astype(BF16)
     c_rope = local(rope_hbm, rope, lsem.at[3])
-    c_cache = local(cache_hbm, cache, csem.at[0])
+    c_cache = local(cache_hbm, cache, csem)
     c_uv = local(wuv_hbm, wuv, lsem.at[4])
     c_out = local(wout_hbm, wout, lsem.at[5])
 
     pl.semaphore_wait(barrier, len(peers))
     def give_z():
         for j in (3, 2, 1):
-            remote(zq.at[z], zq.at[z], q_s.at[0], q_r.at[z], dev_z[j]).start()
+            remote(zq.at[z], zq.at[z], q_s, q_r.at[z], dev_z[j]).start()
 
     give_z()
     pick = onehot((16, 16), lambda i, j: 4 * z + i == j)
@@ -164,7 +164,7 @@
     c_uk.wait()
     latent(z)
     for j in (1, 2, 3):
-        remote(zq.at[zx[j]], zq.at[zx[j]], q_s.at[0], q_r.at[zx[j]], dev_p).wait_recv()
+        remote(zq.at[zx[j]], zq.at[zx[j]], q_s, q_r.at[zx[j]], dev_p).wait_recv()
         latent(zx[j])
     qp = mm(perm, xq[...].reshape(256, QW)).astype(BF16)
     def give(u):
@@ -216,19 +216,19 @@
             acc[u, p, 128:136] = pack([m[cut] for m in ms], [l[cut] for l in ls])
 
     def d_copy(u):
-        return remote(acc.at[u, pl.ds(2, 2)], racc.at[u], d_s.at[0], d_r.at[u], dev_p)
+        return remote(acc.at[u, pl.ds(2, 2)], racc.at[u], d_s, d_r.at[u], dev_p)
 
     def y_copy(u):
-        return remote(acc.at[u, 1], yra.at[u], y_s.at[0], y_r.at[u], dev_y)
+        return remote(acc.at[u, 1], yra.at[u], y_s, y_r.at[u], dev_y)
 
     def z_copy(u):
         n, h = u // 2, u % 2
         to = zx[1] if n == 2 else inner * gs[n] + (1 - inner) * zx[1]
         at = 2 if n == 2 else inner * 3 + (1 - inner) * n
-        return remote(acc.at[u, 0], zra.at[at, h], z_s.at[0], z_r.at[at, h], (x, to, s))
+        return remote(acc.at[u, 0], zra.at[at, h], z_s, z_r.at[at, h], (x, to, s))
 
     def z_wait(at, h):
-        remote(zra.at[at, h], zra.at[at, h], z_s.at[0], z_r.at[at, h], dev_p).wait_recv()
+        remote(zra.at[at, h], zra.at[at, h], z_s, z_r.at[at, h], dev_p).wait_recv()
 
     def add(u, n, other):
         out, m, l = merge([acc[u, n], other])
@@ -281,21 +281,22 @@
     plan = [(-1, stage_r, 0), (0.1, stage_r, 1), (0.4, stage_r, 2)]
     first = {(stage_a, 1): 0.2, (stage_y, 0): 0.3, (stage_y, 1): 0.5}
     for u in range(8):
-        at = PACE * (u + 5) if u < 4 else 1.47 * u + 4.9
+        at = PACE * (u + 5) if u < 4 else 1.47 * u + 3.9
         plan += [(PACE * u, stage_a, u), (PACE * (u + 1) + (0.1 if u else -0.9), stage_y, u), (at, stage_z, u)]
         if u < 4:
-            plan.append((at + 3.6, stage_c, u))
+            plan.append((at + LAG, stage_c, u))
     for _, stage, u in sorted(plan, key=lambda e: first.get(e[1:], e[0])):
         stage(u)
 
-    for at in (2, 3):
-        for h in range(2):
-            z_wait(at, h)
     c_uv.wait()
     c_out.wait()
     ol = []
     for h in range(2):
         u = 6 + h
+        z_wait(2, h)
+        z_wait(3, h)
+        if h:
+            pass
         out, m, l = merge([acc[u, 0], zra[2, h], zra[3, h]])
         ol += [jnp.concatenate([(out[4 * i + c] / l[i]).astype(BF16) for c in range(4)], axis=1) for i in range(2)]
     ol = jnp.concatenate(ol, axis=0)
@@ -311,10 +312,10 @@
         return mm(v, wout[:, :, c * QUART:(c + 1) * QUART].reshape(HLOC * VAL, QUART))[0:4]
 
     def e_copy(c):
-        return remote(yb.at[c], yr.at[c % 2], e_s.at[0], e_r.at[c % 2], dev_p)
+        return remote(yb.at[c], yr.at[c % 2], e_s, e_r.at[c % 2], dev_p)
 
     def t_copy(n):
-        return remote(tr.at[0, n], tr.at[1, n], t_s.at[0], t_r.at[n], dev_y)
+        return remote(tr.at[0, n], tr.at[1, n], t_s, t_r.at[n], dev_y)
 
     def pair(c):
         n = c % 2
@@ -328,8 +329,8 @@
         res = hsel[:, pl.ds(pl.multiple_of(c * QUART, QUART), QUART)] + (tr[0, n] + tr[1, n])
         fin[4 * z + c] = res.astype(BF16)
         for j in (3, 2, 1):
-            go(remote(fin.at[4 * z + c], fin.at[4 * z + c], f_s.at[0], f_r.at[n, j], dev_z[j]))
-        go(remote(fin.at[4 * z + c], fin.at[4 * z + c], f_s.at[0], f_r.at[n, 0], dev_p))
+            go(remote(fin.at[4 * z + c], fin.at[4 * z + c], f_s, f_r.at[n, j], dev_z[j]))
+        go(remote(fin.at[4 * z + c], fin.at[4 * z + c], f_s, f_r.at[n, 0], dev_p))
 
     for c in range(4):
         yb[c] = cols(c)
@@ -346,19 +347,19 @@
     for n in range(2):
         for j in (1, 2, 3):
             at = fin.at[4 * zx[j] + 2 * k + n]
-            remote(at, at, f_s.at[0], f_r.at[n, j], dev_p).wait_recv()
-            go(remote(at, at, f_s.at[0], f_r.at[n, 3 + j], dev_p))
+            remote(at, at, f_s, f_r.at[n, j], dev_p).wait_recv()
+            go(remote(at, at, f_s, f_r.at[n, 3 + j], dev_p))
     for n in range(2):
         for j, zz in enumerate((z, zx[1], zx[2], zx[3])):
             at = fin.at[4 * zz + 2 * (1 - k) + n]
-            remote(at, at, f_s.at[0], f_r.at[n, 3 + j if j else 0], dev_p).wait_recv()
+            remote(at, at, f_s, f_r.at[n, 3 + j if j else 0], dev_p).wait_recv()
     for i in range(4):
         for c in range(4):
             outf[4 * i:4 * i + 4, c * QUART:(c + 1) * QUART] = fin[4 * i + c].astype(F32)
     out_ref[...] = outf[...].astype(BF16)
-    for src, sem in ((zq.at[pl.ds(0, 3)], q_s.at[0]), (qg.at[:, 0], a_s.at[0]), (qg.at[:, 0], a_s.at[1]), (qg.at[:, 1], a_s.at[2]),
-                     (acc.at[:, pl.ds(2, 2)], d_s.at[0]), (acc.at[:, 1], y_s.at[0]), (acc.at[pl.ds(0, 6), 0], z_s.at[0]),
-                     (yb.at[pl.ds(0, 2)], e_s.at[0]), (tr.at[0], t_s.at[0]), (fin.at[pl.ds(0, 14)], f_s.at[0])):
+    for src, sem in ((zq.at[pl.ds(0, 3)], q_s), (qg.at[:, 0], a_s.at[0]), (qg.at[:, 0], a_s.at[1]), (qg.at[:, 1], a_s.at[2]),
+                     (acc.at[:, pl.ds(2, 2)], d_s), (acc.at[:, 1], y_s), (acc.at[pl.ds(0, 6), 0], z_s),
+                     (yb.at[pl.ds(0, 2)], e_s), (tr.at[0], t_s), (fin.at[pl.ds(0, 14)], f_s)):
         remote(src, src, sem, d_r.at[0], dev_p).wait_send()
 
 
@@ -372,7 +373,7 @@
             pltpu.VMEM((ROWS, D), BF16),
             pltpu.VMEM((ROWS, TLOC, LAT), BF16),
             pltpu.VMEM((ROWS, ROPE, TLOC), BF16),
-            pltpu.VMEM((NCH, CH, 4, NOPE), BF16),
+            pltpu.VMEM((NCH // 2, 2 * CH, 4, NOPE), BF16),
             pltpu.VMEM((4, ROPE, D), BF16),
             pltpu.VMEM((HLOC, NOPE, LAT), BF16),
             pltpu.VMEM((HLOC, LAT, VAL), BF16),
@@ -392,14 +393,14 @@
             pltpu.VMEM((16, 4, QUART), BF16),
             pltpu.VMEM((4, D), F32),
             pltpu.VMEM((ROWS, D), F32),
-            dma((6,)), dma((NCH,)), dma((1,)),
-            dma((1,)), dma((4,)),
+            dma((6,)), dma((2,)), dma,
+            dma, dma((4,)),
             dma((3,)), dma((8, 3)),
-            dma((1,)), dma((8,)),
-            dma((1,)), dma((8,)),
-            dma((1,)), dma((4, 2)),
-            dma((1,)), dma((2,)), dma((1,)), dma((2,)),
-            dma((1,)), dma((2, 7)),
+            dma, dma((8,)),
+            dma, dma((8,)),
+            dma, dma((4, 2)),
+            dma, dma((2,)), dma, dma((2,)),
+            dma, dma((2, 7)),
         ]
         return pl.pallas_call(
             kernel,

time: 49.7 us -> 49.5 us (level)
  no operation moved by 1% of the time
where the time goes in v6:
time: 49.5 us; the launch traced here: 49.4 us
  Pallas kernels  48.7 us (98%)
  local copies, waits for them, and re-layouts  0.68 us (1%)
    pallas_call x1, Pallas kernels, local_step(): pl.pallas_call(kernel, out_shape=pltpu.VMEM((ROWS, D), BF16), in_specs=[p...  48.7 us

profile of v6, /device:TPU:0, one launch (start us, length us, event | category | flops | bytes accessed | tf_op | source)
XLA Modules:
  0.0 49.4 jit_solution(5134307897675001832)
XLA Ops:
  0.0 48.7 %shard_map.91 = bf16[16,6144]{1,0:T(8,128)(2,1)S(1)} custom-call(s32[16]{0:T(128)} %len_ref.1, bf16[16,6144]{1,0:T(8,128)(2,1)} %hid_hbm.1, bf16[16,512,512]{2,1,0:T(8,128)(2,1)} %cache_hbm.1, bf16[16,64,512]{2,1,0:T(8,128)(2,1)} %bitcast.3, bf16[6144,16,128]{2,1,0:T(8,128)(2,1)} %wuq_hbm.1, bf16[16,64,6144]{2,1,0:T(8,128)(2,1)} %bitcast.2, ...), custom_call_target="tpu_custom_call" | custom-call | tf_op jit(solution)/shard_map/pallas_call | solution.py:405
  48.7 0.7 %copy.11 = bf16[16,6144]{1,0:T(8,128)(2,1)} copy(bf16[16,6144]{1,0:T(8,128)(2,1)S(1)} %shard_map.91) | data formatting | bytes 393216

commit v7 on v6

--- a/solution.py
+++ b/solution.py
@@ -18,6 +18,7 @@
 NCH = D // CH
 BLK = CH // 128
 QUART = D // 4
+PAIR = 2
 PACE = 1.2
 LAG = 3.6
 AHEAD = 5
@@ -78,7 +79,9 @@
     spy = sp + 2 - 4 * y
     zx = {1: z + 1 - 2 * (z % 2), 2: z + 2 - 4 * (z // 2), 3: 3 - z}
     inner = ((z + 1) // 2) % 2
-    gs = [3 * (1 - z // 2), 2 - z // 2, zx[1], z]
+    far = [3 * (1 - z // 2), 2 - z // 2]
+    outer = 1 - inner
+    gs = [inner * zx[1] + outer * far[0], inner * far[0] + outer * far[1], inner * far[1] + outer * zx[1], z]
 
     dev_p, dev_y = (x, z, sp), (x, z, sy)
     dev_z = {j: (x, zx[j], s) for j in zx}
@@ -172,7 +175,10 @@
         go(remote(qg.at[u, 0], qg.at[u, 2], a_s.at[1], a_r.at[u, 1], dev_p))
 
     for u in range(8):
-        qg[u, 0] = qp[32 * u:32 * u + 32]
+        rows = qp[32 * u:32 * u + 32]
+        for c in range(4):
+            qg[u, 0, 32 * c:32 * c + 32] = rows[:, NOPE * c:NOPE * c + NOPE]
+        qg[u, 0, NOPE:] = jnp.concatenate([rows[:16, LAT:LAT + ROPE], rows[16:, LAT:LAT + ROPE]], axis=1)
         if u < AHEAD:
             give(u)
 
@@ -189,18 +195,19 @@
     t0 = (z * 4 + s) * TLOC
 
     def rows_of(u):
-        return [4 * gs[u // 2] + 2 * (u % 2) + i for i in range(2)]
+        return [4 * gs[u // PAIR] + 2 * (u % PAIR) + i for i in range(2)]
 
     def scores(u):
         for i, b in enumerate(rows_of(u)):
-            q = jnp.concatenate([qg[u, p, 16 * i:16 * i + 16, :] for p in range(4)], axis=0)
-            sbuf[u % 2, i] = mm_nt(q[:, :LAT], cache[b]) + mm(q[:, LAT:LAT + ROPE], rope[b])
+            q = [jnp.concatenate([qg[u, p, 32 * c + 16 * i:32 * c + 16 * i + 16] for p in range(4)], axis=0) for c in range(4)]
+            r = jnp.concatenate([qg[u, p, NOPE:] for p in range(4)], axis=0)[:, ROPE * i:ROPE * i + ROPE]
+            sbuf[u % PAIR, i] = mm_nt(jnp.concatenate(q, axis=1), cache[b]) + mm(r, rope[b])
 
     def attend(u):
         ws, ms, ls = [], [], []
         for i, b in enumerate(rows_of(u)):
             valid = lax.broadcasted_iota(jnp.int32, (64, TLOC), 1) < len_ref[b] - t0
-            v = jnp.where(valid, sbuf[u % 2, i] * scale, NEG)
+            v = jnp.where(valid, sbuf[u % PAIR, i] * scale, NEG)
             m = jnp.max(v, axis=1, keepdims=True)
             w = jnp.where(valid, jnp.exp(v - m), 0.0)
             ms.append(m)
@@ -222,9 +229,9 @@
         return remote(acc.at[u, 1], yra.at[u], y_s, y_r.at[u], dev_y)
 
     def z_copy(u):
-        n, h = u // 2, u % 2
-        to = zx[1] if n == 2 else inner * gs[n] + (1 - inner) * zx[1]
-        at = 2 if n == 2 else inner * 3 + (1 - inner) * n
+        n, h = u // PAIR, u % PAIR
+        to = inner * gs[n] + outer * zx[1]
+        at = inner * (3 if n else 2) + outer * n
         return remote(acc.at[u, 0], zra.at[at, h], z_s, z_r.at[at, h], (x, to, s))
 
     def z_wait(at, h):
@@ -261,18 +268,16 @@
     def stage_z(u):
         y_copy(u).wait_recv()
         add(u, 0, yra[u])
-        if u < 4:
-            @pl.when(inner == 0)
-            def _():
-                z_copy(u).start()
+        if u < 2:
+            go(z_copy(u))
         elif u < 6:
-            go(z_copy(u))
+            pl.when(inner == 0)(lambda: z_copy(u).start())
 
     def stage_c(u):
         @pl.when(inner == 1)
         def _():
-            z_wait(u // 2, u % 2)
-            add(u, 0, zra[u // 2, u % 2])
+            z_wait(u // PAIR - 1, u % PAIR)
+            add(u, 0, zra[u // PAIR - 1, u % PAIR])
             z_copy(u).start()
 
     forward(0)
@@ -284,7 +289,7 @@
         at = PACE * (u + 5) if u < 4 else 1.47 * u + 3.9
         plan += [(PACE * u, stage_a, u), (PACE * (u + 1) + (0.1 if u else -0.9), stage_y, u), (at, stage_z, u)]
         if u < 4:
-            plan.append((at + LAG, stage_c, u))
+            plan.append((at + LAG, stage_c, u + 2))
     for _, stage, u in sorted(plan, key=lambda e: first.get(e[1:], e[0])):
         stage(u)
 
@@ -381,7 +386,7 @@
             pltpu.VMEM((48, 16, 512), BF16),
             pltpu.VMEM((4, 96, 128), BF16),
             pltpu.VMEM((HLOC, 16, QW), BF16),
-            pltpu.VMEM((8, 4, 32, QW), BF16),
+            pltpu.VMEM((8, 4, 144, NOPE), BF16),
             pltpu.VMEM((2, 2, 64, TLOC), F32),
             pltpu.VMEM((8, 4, 136, 128), F32),
             pltpu.VMEM((8, 2, 136, 128), F32),

time: 49.5 us -> 49.3 us (level)
  no operation moved by 1% of the time
where the time goes in v7:
time: 49.3 us; the launch traced here: 49.2 us
  Pallas kernels  48.5 us (98%)
  local copies, waits for them, and re-layouts  0.68 us (1%)
    pallas_call x1, Pallas kernels, local_step(): pl.pallas_call(kernel, out_shape=pltpu.VMEM((ROWS, D), BF16), in_specs=[p...  48.5 us

profile of v7, /device:TPU:0, one launch (start us, length us, event | category | flops | bytes accessed | tf_op | source)
XLA Modules:
  0.0 49.2 jit_solution(9185938468033403255)
XLA Ops:
  0.0 48.5 %shard_map.91 = bf16[16,6144]{1,0:T(8,128)(2,1)S(1)} custom-call(s32[16]{0:T(128)} %len_ref.1, bf16[16,6144]{1,0:T(8,128)(2,1)} %hid_hbm.1, bf16[16,512,512]{2,1,0:T(8,128)(2,1)} %cache_hbm.1, bf16[16,64,512]{2,1,0:T(8,128)(2,1)} %bitcast.3, bf16[6144,16,128]{2,1,0:T(8,128)(2,1)} %wuq_hbm.1, bf16[16,64,6144]{2,1,0:T(8,128)(2,1)} %bitcast.2, ...), custom_call_target="tpu_custom_call" | custom-call | tf_op jit(solution)/shard_map/pallas_call | solution.py:410
  48.5 0.7 %copy.11 = bf16[16,6144]{1,0:T(8,128)(2,1)} copy(bf16[16,6144]{1,0:T(8,128)(2,1)S(1)} %shard_map.91) | data formatting | bytes 393216

commit v8 on v7

--- a/solution.py
+++ b/solution.py
@@ -266,11 +266,13 @@
         add(u, 0, racc[u, 0])
 
     def stage_z(u):
+        if u == 5:
+            pl.when(inner == 0)(lambda: z_copy(u - 1).start())
         y_copy(u).wait_recv()
         add(u, 0, yra[u])
         if u < 2:
             go(z_copy(u))
-        elif u < 6:
+        elif u in (2, 3, 5):
             pl.when(inner == 0)(lambda: z_copy(u).start())
 
     def stage_c(u):

time: 49.3 us -> 49.3 us (level)
  no operation moved by 1% of the time
where the time goes in v8:
time: 49.3 us; the launch traced here: 49.2 us
  Pallas kernels  48.5 us (98%)
  local copies, waits for them, and re-layouts  0.68 us (1%)
    pallas_call x1, Pallas kernels, local_step(): pl.pallas_call(kernel, out_shape=pltpu.VMEM((ROWS, D), BF16), in_specs=[p...  48.5 us

profile of v8, /device:TPU:0, one launch (start us, length us, event | category | flops | bytes accessed | tf_op | source)
XLA Modules:
  0.0 49.2 jit_solution(10004987226738278689)
XLA Ops:
  0.0 48.5 %shard_map.91 = bf16[16,6144]{1,0:T(8,128)(2,1)S(1)} custom-call(s32[16]{0:T(128)} %len_ref.1, bf16[16,6144]{1,0:T(8,128)(2,1)} %hid_hbm.1, bf16[16,512,512]{2,1,0:T(8,128)(2,1)} %cache_hbm.1, bf16[16,64,512]{2,1,0:T(8,128)(2,1)} %bitcast.3, bf16[6144,16,128]{2,1,0:T(8,128)(2,1)} %wuq_hbm.1, bf16[16,64,6144]{2,1,0:T(8,128)(2,1)} %bitcast.2, ...), custom_call_target="tpu_custom_call" | custom-call | tf_op jit(solution)/shard_map/pallas_call | solution.py:412
  48.5 0.7 %copy.11 = bf16[16,6144]{1,0:T(8,128)(2,1)} copy(bf16[16,6144]{1,0:T(8,128)(2,1)S(1)} %shard_map.91) | data formatting | bytes 393216
